TPU v7x, 256 devices: a whole 4x4x8 slice. The times are simulated.
256 devices in a mesh: epoch: 16 (over y, x), blend: 16 (over z, core).
Axes of the slice: x: 4, y: 4, z: 8, core: 2. Of those that a mesh axis runs over, the one named last changes fastest.
Arguments:
- visit_flux: bfloat16 [64, 64, 6, 16384], P('epoch', None, None, 'blend'), may hold values from -6 to 6
- visit_precision: bfloat16 [64, 64, 6, 16384], P('epoch', None, None, 'blend'), may hold values from 0.25 to 4
- visit_live: int32 [64, 64], P('epoch'), may hold values 0 or 1
- footprint: int32 [64, 8, 16384], P('blend', None, 'epoch'), may hold values 0 or 1
- source_count: int32 [64], P('blend'), may hold values from 1 to 8
- spectra_init: float32 [64, 8, 6], P('blend'), may hold values from 0.2 to 1.2
- morphology_init: float32 [64, 8, 16384], P('blend', None, 'epoch'), may hold values from 0 to 0.25
Outputs:
- coadd_flux: float32 [64, 6, 16384], P('blend', None, 'epoch')
- spectra: float32 [64, 8, 6], P('blend')
- morphology: float32 [64, 8, 16384], P('blend', None, 'epoch')
All inputs are finite; a program needn't handle non-finite values. No bound on the sum of `visit_live` or of `footprint` on one device may be relied on, other than what follows from the above.
Results may differ from a plain program's by a relative error of at most 0.0003.
Values sent between devices are 32-bit elements; how exact they have to be, the bound alone decides.
A program may use at most 64 MiB of HBM per device.

v0:
```python
import jax
import jax.numpy as jnp
from jax import lax
from jax.sharding import PartitionSpec as P

ITERS = 2


def in_blocks(array, dim, count):
    shape = array.shape
    pieces = array.reshape(*shape[:dim], count, shape[dim] // count, *shape[dim + 1 :])
    return jnp.moveaxis(pieces, dim, 0)


def sent_and_summed(array, axis, dim):
    pieces = in_blocks(array, dim, lax.axis_size(axis))
    arrived = lax.all_to_all(pieces, axis, split_axis=0, concat_axis=0, tiled=True)
    return arrived.sum(axis=0)


def side_by_side(arrays, axis, dim, along):
    widths = [a.shape[along] for a in arrays]
    both = jnp.concatenate(arrays, axis=along)
    filled = sent_and_summed(both, axis, dim)
    return tuple(jnp.split(filled, [sum(widths[:k]) for k in range(1, len(widths))], axis=along))


def side_by_side_2(arrays, axis, split_dim, concat_dim, along):
    widths = [a.shape[along] for a in arrays]
    both = jnp.concatenate(arrays, axis=along)
    filled = lax.all_to_all(both, axis, split_axis=split_dim, concat_axis=concat_dim, tiled=True)
    return tuple(jnp.split(filled, [sum(widths[:k]) for k in range(1, len(widths))], axis=along))


def from_everyone(array, axis):
    copies = jnp.broadcast_to(array, (lax.axis_size(axis), *array.shape))
    return lax.all_to_all(copies, axis, split_axis=0, concat_axis=0, tiled=True)


def of_everyone(array, axis):
    return from_everyone(array, axis).sum(axis=0)


def together(arrays, axis):
    line, at, finished = (jnp.concatenate([a.reshape(-1) for a in arrays]), 0, [])
    subtotal = of_everyone(line, axis)
    for a in arrays:
        finished.append(subtotal[at : at + a.size].reshape(a.shape))
        at += a.size
    return tuple(finished)


def on_device(
    visit_flux, visit_precision, visit_live, footprint, source_count, spectra_init, morphology_init
):
    weights = visit_precision.astype(jnp.float32) * visit_live.astype(jnp.float32)[:, :, None, None]
    numerator = jnp.sum(weights * visit_flux.astype(jnp.float32), axis=0)
    weight_sum = jnp.sum(weights, axis=0)
    pix_part = morphology_init.shape[2]
    owned = morphology_init.shape[0]
    numerator, weight_sum = side_by_side((numerator, weight_sum), "epoch", 2, 0)
    every_blend, band_count, piece = numerator.shape
    numerator = numerator.reshape(every_blend, band_count, 1, piece)
    weight_sum = weight_sum.reshape(every_blend, band_count, 1, piece)
    numerator, weight_sum = side_by_side_2((numerator, weight_sum), "blend", 0, 2, 1)
    blocks = numerator.shape[2]
    numerator = numerator.reshape(owned, band_count, blocks, 1, piece)
    weight_sum = weight_sum.reshape(owned, band_count, blocks, 1, piece)
    numerator, weight_sum = side_by_side_2((numerator, weight_sum), "epoch", 2, 3, 0)
    numerator = numerator.reshape(owned, band_count, pix_part)
    weight_sum = weight_sum.reshape(owned, band_count, pix_part)
    coadd_flux = numerator / (1.0 + weight_sum)
    coverage = weight_sum / (1.0 + weight_sum)
    slots = footprint.shape[1]
    source_live = (jnp.arange(slots, dtype=jnp.int32)[None, :] < source_count[:, None]).astype(
        jnp.float32
    )
    footprint_mask = footprint.astype(jnp.float32) * source_live[:, :, None]
    live_count = source_count.astype(jnp.float32)
    morphology = morphology_init * footprint_mask
    spectra = spectra_init
    highest = lax.Precision.HIGHEST
    for iteration in range(ITERS):
        blend_model = jnp.einsum("bkc,bkp->bcp", spectra, morphology, precision=highest)
        residual = coverage * (coadd_flux - blend_model)
        morph_grad = jnp.einsum("bkc,bcp->bkp", spectra, residual, precision=highest)
        morph_step = 1.0 / (1.0 + live_count[:, None] * jnp.sum(spectra * spectra, axis=2))
        morphology = (
            jnp.maximum(0.0, morphology + morph_grad * morph_step[:, :, None]) * footprint_mask
        )
        blend_model = jnp.einsum("bkc,bkp->bcp", spectra, morphology, precision=highest)
        residual = coverage * (coadd_flux - blend_model)
        spectra_grad = jnp.einsum("bkp,bcp->bkc", morphology, residual, precision=highest)
        morph_norm = jnp.sum(morphology * morphology, axis=2)
        spectra_grad, morph_norm = together((spectra_grad, morph_norm), "epoch")
        spectra = jnp.maximum(
            0.0, spectra + spectra_grad / (1.0 + live_count[:, None] * morph_norm)[:, :, None]
        )
    return (coadd_flux, spectra, morphology)


def solution(mesh):
    in_specs = (
        P("epoch", None, None, "blend"),
        P("epoch", None, None, "blend"),
        P("epoch", None),
        P("blend", None, "epoch"),
        P("blend"),
        P("blend", None, None),
        P("blend", None, "epoch"),
    )
    out_specs = (P("blend", None, "epoch"), P("blend", None, None), P("blend", None, "epoch"))
    return jax.shard_map(
        on_device, mesh=mesh, in_specs=in_specs, out_specs=out_specs, check_vma=False
    )
```

profile of v0, /device:TPU:1, one launch (start us, length us, event | category | flops | bytes accessed | tf_op | source)
XLA Modules:
  0.0 121.1 jit_solution(499427961824183499)
XLA Ops:
  0.6 0.7 convert_element_type.23
  1.3 5.1 %multiply_reduce_fusion = (f32[64,6,1024]{2,0,1:T(8,128)S(1)}, f32[64,6,1024]{2,0,1:T(8,128)S(1)}) fusion(bf16[4,64,6,1024]{3,1,2,0:T(8,128)(2,1)} %param.7, bf16[4,64,6,1024]{3,1,2,0:T(8,128)(2,1)} %param.8, f32[4,64]{1,0:T(4,128)S(1)} %convert_element_type.23), kind=kLoop, calls=%fused_computation | loop fusion | flops 8650752 | bytes 9438208 | tf_op jit(solution)/shard_map/reduce_sum | solution.py:57
  6.4 0.2 pad_maximum_fusion
  6.6 2.4 %copy.93 = f32[128,6,1024]{0,2,1:T(8,128)} copy(f32[128,6,1024]{2,0,1:T(8,128)S(1)} %pad_maximum_fusion) | data formatting | bytes 6291456 | tf_op jit(solution)/shard_map/concatenate | solution.py:23
  9.0 2.1 %copy.94 = f32[16,128,6,64]{1,3,2,0:T(8,128)S(1)} copy(f32[16,128,6,64]{1,3,0,2:T(8,128)} %bitcast.62) | data formatting | bytes 6291456 | tf_op jit(solution)/shard_map/transpose | solution.py:12
  11.1 45.9 %all_to_all.44 = f32[16,128,6,64]{1,3,2,0:T(8,128)S(1)} all-to-all(f32[16,128,6,64]{1,3,2,0:T(8,128)S(1)} %copy.94), channel_id=1, replica_groups=mesh['epoch'=16,'blend'=16] {'epoch'}, dimensions={0} | all-to-all | bytes 6291456 | tf_op jit(solution)/shard_map/all_to_all | solution.py:17
  57.0 0.2 reduce_sum.83
  57.2 0.1 slice_bitcast_fusion.3
  57.4 0.5 broadcast.129
  57.9 0.7 reduce.2
  58.6 0.3 copy.134
  58.9 0.9 reshape.200
  59.8 10.5 %all-to-all-start.1 = ((f32[16,1,3072]{2,1,0:T(1,128)}), f32[16,1,3072]{2,1,0:T(1,128)S(1)}, u32[]{:S(2)}, u32[]{:S(2)}) async-start(f32[16,1,3072]{2,1,0:T(1,128)} %reshape.200), calls=%async_computation.1 | async-start | bytes 393216 | tf_op jit(solution)/shard_map/all_to_all | solution.py:31
  70.4 0.1 copy.108
  70.6 10.0 %all-to-all-done.1 = f32[16,1,3072]{2,1,0:T(1,128)S(1)} async-done(((f32[16,1,3072]{2,1,0:T(1,128)}), f32[16,1,3072]{2,1,0:T(1,128)S(1)}, u32[]{:S(2)}, u32[]{:S(2)}) %all-to-all-start.1) | async-done | bytes 196640 | tf_op jit(solution)/shard_map/all_to_all | solution.py:31
  80.5 1.1 reduce.3
  81.7 0.5 reshape.201
  82.2 0.1 copy_bitcast_fusion
  82.3 0.9 reshape.202
  83.2 3.5 %all-to-all-start.2 = ((f32[16,1,3072]{2,1,0:T(1,128)}), f32[16,1,3072]{2,1,0:T(1,128)S(1)}, u32[]{:S(2)}, u32[]{:S(2)}) async-start(f32[16,1,3072]{2,1,0:T(1,128)} %reshape.202), calls=%async_computation.2 | async-start | bytes 393216 | tf_op jit(solution)/shard_map/all_to_all | solution.py:31
  86.8 7.9 %all-to-all-done.2 = f32[16,1,3072]{2,1,0:T(1,128)S(1)} async-done(((f32[16,1,3072]{2,1,0:T(1,128)}), f32[16,1,3072]{2,1,0:T(1,128)S(1)}, u32[]{:S(2)}, u32[]{:S(2)}) %all-to-all-start.2) | async-done | bytes 196640 | tf_op jit(solution)/shard_map/all_to_all | solution.py:31
  94.7 1.1 reduce.4
  95.8 0.1 reshape.203
  96.1 0.1 reshape.199
  96.2 0.1 reshape.198
  96.4 0.3 fusion.4
  96.7 0.3 multiply_reduce_fusion.2
  97.1 0.3 fusion.8
  97.3 0.3 fusion.21
  97.7 0.1 reshape.190
  97.8 0.1 reshape.191
  98.0 9.2 %all_to_all.45 = f32[16,1,224]{2,1,0:T(1,128)S(1)} all-to-all(f32[16,1,224]{2,1,0:T(1,128)S(1)} %broadcast_in_dim.4), channel_id=1, replica_groups=mesh['epoch'=16,'blend'=16] {'epoch'}, dimensions={0} | all-to-all | bytes 28672 | tf_op jit(solution)/shard_map/all_to_all | solution.py:37
  107.3 0.1 reshape.192
  107.4 0.1 reshape.193
  107.5 0.2 multiply_reduce_fusion.3
  107.7 0.3 fusion.9
  108.1 0.4 multiply_reduce_fusion.1
  108.5 0.3 fusion.13
  108.8 0.3 fusion.22
  109.2 0.1 reshape.194
  109.3 0.1 reshape.195
  109.4 0.6 broadcast_in_dim.5
  110.1 3.5 %all-to-all-start.4 = ((f32[16,1,224]{2,1,0:T(1,128)}), f32[16,1,224]{2,1,0:T(1,128)S(1)}, u32[]{:S(2)}, u32[]{:S(2)}) async-start(f32[16,1,224]{2,1,0:T(1,128)} %broadcast_in_dim.5), calls=%async_computation.4 | async-start | bytes 32768 | tf_op jit(solution)/shard_map/all_to_all | solution.py:37
  113.6 0.7 copy.112
  114.3 5.7 %all-to-all-done.4 = f32[16,1,224]{2,1,0:T(1,128)S(1)} async-done(((f32[16,1,224]{2,1,0:T(1,128)}), f32[16,1,224]{2,1,0:T(1,128)S(1)}, u32[]{:S(2)}, u32[]{:S(2)}) %all-to-all-start.4) | async-done | bytes 14368 | tf_op jit(solution)/shard_map/all_to_all | solution.py:37
  120.0 0.1 reshape.196
  120.3 0.1 add_maximum_fusion
  120.4 0.7 copy.113
  (32 shorter events, 1.1 us)
Async XLA Ops:
  57.0 13.3 %copy-start.4 = (s32[4]{0:T(128)S(1)}, s32[4]{0:T(128)}, u32[]{:S(2)}) copy-start(s32[4]{0:T(128)} %param.11) | copy-start | bytes 52
  57.0 13.3 %copy-start.3 = (f32[4,8,6]{1,0,2:T(4,128)S(1)}, f32[4,8,6]{1,0,2:T(4,128)}, u32[]{:S(2)}) copy-start(f32[4,8,6]{1,0,2:T(4,128)} %param.12) | copy-start | bytes 2308
  59.8 20.7 %all-to-all-start.1 = ((f32[16,1,3072]{2,1,0:T(1,128)}), f32[16,1,3072]{2,1,0:T(1,128)S(1)}, u32[]{:S(2)}, u32[]{:S(2)}) async-start(f32[16,1,3072]{2,1,0:T(1,128)} %reshape.200), calls=%async_computation.1 | async-start | bytes 393216 | tf_op jit(solution)/shard_map/all_to_all | solution.py:31
  82.2 14.2 %copy-start.1 = (s32[4,8,1024]{2,1,0:T(8,128)S(1)}, s32[4,8,1024]{2,1,0:T(8,128)}, u32[]{:S(2)}) copy-start(s32[4,8,1024]{2,1,0:T(8,128)} %param.10) | copy-start | bytes 393220
  82.2 14.2 %copy-start.2 = (f32[4,8,1024]{2,1,0:T(8,128)S(1)}, f32[4,8,1024]{2,1,0:T(8,128)}, u32[]{:S(2)}) copy-start(f32[4,8,1024]{2,1,0:T(8,128)} %param.13) | copy-start | bytes 393220
  83.2 11.5 %all-to-all-start.2 = ((f32[16,1,3072]{2,1,0:T(1,128)}), f32[16,1,3072]{2,1,0:T(1,128)S(1)}, u32[]{:S(2)}, u32[]{:S(2)}) async-start(f32[16,1,3072]{2,1,0:T(1,128)} %reshape.202), calls=%async_computation.2 | async-start | bytes 393216 | tf_op jit(solution)/shard_map/all_to_all | solution.py:31
  108.5 12.6 %copy-start = (f32[4,8,1024]{2,1,0:T(8,128)}, f32[4,8,1024]{2,1,0:T(8,128)S(1)}, u32[]{:S(2)}) copy-start(f32[4,8,1024]{2,1,0:T(8,128)S(1)} %get-tuple-element.34) | copy-start | bytes 393220
  110.1 9.9 %all-to-all-start.4 = ((f32[16,1,224]{2,1,0:T(1,128)}), f32[16,1,224]{2,1,0:T(1,128)S(1)}, u32[]{:S(2)}, u32[]{:S(2)}) async-start(f32[16,1,224]{2,1,0:T(1,128)} %broadcast_in_dim.5), calls=%async_computation.4 | async-start | bytes 32768 | tf_op jit(solution)/shard_map/all_to_all | solution.py:37
where the time goes:
time: 123 us; the launch traced here: 121 us
  blocking collectives  55.1 us (45%)
  waiting for transfers between devices  23.5 us (19%)
  starting transfers between devices  17.6 us (14%)
  local copies, waits for them, and re-layouts  11.3 us (9%)
  other arithmetic  10.1 us (8%)
  matrix products  2.63 us (2%)
    all_to_all x1, blocking collectives, sent_and_summed(): lax.all_to_all(pieces, axis, split_axis=0, concat_axis=0, tiled=True)  45.9 us
    all_to_all x2, waiting for transfers between devices, side_by_side_2(): lax.all_to_all(both, axis, split_axis=split_dim, concat_axis=concat_dim,...  17.9 us
    all_to_all x2, starting transfers between devices, side_by_side_2(): lax.all_to_all(both, axis, split_axis=split_dim, concat_axis=concat_dim,...  14.1 us
    all_to_all x1, blocking collectives, from_everyone(): return lax.all_to_all(copies, axis, split_axis=0, concat_axis=0, tiled=True)  9.19 us
    all_to_all x1, waiting for transfers between devices, from_everyone(): return lax.all_to_all(copies, axis, split_axis=0, concat_axis=0, tiled=True)  5.67 us
    reduce_sum x1, other arithmetic, on_device(): numerator = jnp.sum(weights * visit_flux.astype(jnp.float32), axis=0)  5.1 us
    unnamed x18, local copies, waits for them, and re-layouts  4.22 us
    all_to_all x1, starting transfers between devices, from_everyone(): return lax.all_to_all(copies, axis, split_axis=0, concat_axis=0, tiled=True)  3.49 us
  transfers between devices with their start and end apart: 3, of which 3 were waited for; matrix products, arithmetic and copies ran while one was open for 1% of the time, Pallas kernels for 0%

commit v1 on v0

v1 whole, which is shorter than its diff:
```python
import jax
import jax.numpy as jnp
from jax import lax
from jax.experimental import pallas as pl
from jax.experimental.pallas import tpu as pltpu
from jax.sharding import PartitionSpec as P

ITERS = 2
LANES = 128
F32 = jnp.float32
HIGHEST = lax.Precision.HIGHEST


def kernel(
    flux, prec, live, foot, count, spec, morph,
    coadd_o, spec_o, morph_o,
    fx, pr, live_i, live_b, ft, mo, sp_in, sp_s,
    part, rf, rp, rs, red, rf2, rp2, rs2, zs, zr, fin, co, cv, ar,
    load_sem, small_sem, s1, r1, s2, r2, zsem_s, zsem_r, xsem_s, xsem_r, asem_s, asem_r,
):
    e = lax.axis_index("epoch")
    b = lax.axis_index("blend")
    y, x = lax.div(e, 4), lax.rem(e, 4)
    z, c = lax.div(b, 2), lax.rem(b, 2)

    def mod4(v):
        return lax.rem(v, 4)

    order = [
        mod4(x + 2), 4 + mod4(y + 2),
        mod4(x + 1), mod4(x + 3), 4 + mod4(y + 1), 4 + mod4(y + 3),
        x, 4 + y,
    ]

    small = [
        pltpu.make_async_copy(live, live_i, small_sem.at[0]),
        pltpu.make_async_copy(spec, sp_in, small_sem.at[1]),
        pltpu.make_async_copy(foot, ft, small_sem.at[2]),
        pltpu.make_async_copy(morph, mo, small_sem.at[3]),
    ]
    small[0].start()
    loads = []
    for i, t in enumerate(order):
        lanes = pl.ds(pl.multiple_of(t * LANES, LANES), LANES)
        pair = (
            pltpu.make_async_copy(flux.at[:, :, :, lanes], fx.at[i], load_sem.at[0, i]),
            pltpu.make_async_copy(prec.at[:, :, :, lanes], pr.at[i], load_sem.at[1, i]),
        )
        for cp in pair:
            cp.start()
        loads.append(pair)
    for cp in small[1:]:
        cp.start()

    barrier = pltpu.get_barrier_semaphore()
    for d in range(1, 16):
        pl.semaphore_signal(barrier, inc=1, device_id={"epoch": lax.rem(e + d, 16), "blend": b})
        pl.semaphore_signal(barrier, inc=1, device_id={"epoch": e, "blend": lax.rem(b + d, 16)})

    small[0].wait()
    live_f = live_i[...].astype(F32)
    for v in range(4):
        pick = (lax.broadcasted_iota(jnp.int32, (4, LANES), 0) == v).astype(F32)
        live_b[v] = lax.dot_general(
            live_f, pick, (((0,), (0,)), ((), ())), preferred_element_type=F32
        )

    low = lax.broadcasted_iota(jnp.int32, (8, LANES), 0) < 4

    def local_sums(i):
        for cp in loads[i]:
            cp.wait()
        t = order[i]

        def body(g, _):
            rows = pl.ds(pl.multiple_of(g * 16, 16), 16)
            for cpair in range(3):
                sums = []
                for cc in range(2):
                    band = 2 * cpair + cc
                    num = wsum = None
                    for v in range(4):
                        w = pr[i, v, band, rows, :].astype(F32) * live_b[v, rows, :]
                        n = w * fx[i, v, band, rows, :].astype(F32)
                        num = n if num is None else num + n
                        wsum = w if wsum is None else wsum + w
                    sums.append((num, wsum))
                for q in range(2):
                    for zz in range(2):
                        even = sums[0][q][8 * zz : 8 * zz + 8]
                        odd = sums[1][q][8 * zz : 8 * zz + 8]
                        part[t, q, 0, 2 * g + zz, cpair] = jnp.where(low, even, pltpu.roll(odd, 4, 0))
                        part[t, q, 1, 2 * g + zz, cpair] = jnp.where(low, pltpu.roll(even, 4, 0), odd)
            return 0

        lax.fori_loop(0, 4, body, 0)

    def at_x(d):
        return {"epoch": 4 * y + mod4(x + d), "blend": b}

    def at_y(d):
        return {"epoch": 4 * mod4(y + d) + x, "blend": b}

    def rdma(src, dst, ssem, rsem, dev):
        return pltpu.make_async_remote_copy(
            src, dst, ssem, rsem, device_id=dev, device_id_type=pl.DeviceIdType.MESH
        )

    pos1 = (x, y)
    at1 = (at_x, at_y)

    def chunk1(h, d, q):
        return part.at[4 * h + mod4(pos1[h] + d), q]

    def msg1(h, kind, direction):
        d = 1 if direction == 0 else 3
        if kind == 0:
            src, dst = chunk1(h, 2, direction), rf.at[h, direction]
        elif kind == 1:
            src, dst = chunk1(h, d, 1 - direction), rp.at[h, direction]
        else:
            src, dst = chunk1(h, d, direction), rs.at[h, direction]
        n = 6 * h + 2 * kind + direction
        return rdma(src, dst, s1.at[n], r1.at[n], at1[h](d))

    local_sums(0)
    local_sums(1)
    pl.semaphore_wait(barrier, 30)
    for h in range(2):
        for direction in range(2):
            msg1(h, 0, direction).start()
    for i in (2, 3, 4, 5):
        local_sums(i)
        h, direction = (i - 2) // 2, (i - 2) % 2
        msg1(h, 1, direction).start()
    local_sums(6)
    local_sums(7)

    def add_into(dst, *srcs):
        def body(j, _):
            a, m = lax.div(j, 8), lax.rem(j, 8)
            total = dst[a, m]
            for s in srcs:
                total = total + s[a, m]
            dst[a, m] = total
            return 0

        lax.fori_loop(0, 16, body, 0)

    for h in range(2):
        for direction in range(2):
            msg1(h, 0, direction).wait_recv()
            d = 1 if direction == 0 else 3
            add_into(chunk1(h, d, direction), rf.at[h, direction])
            msg1(h, 2, direction).start()

    for cp in small[1:]:
        cp.wait()
    krow = lax.broadcasted_iota(jnp.int32, (8, 1024), 0)
    for j in range(4):
        rows = pl.ds(8 * j, 8)
        seen = (krow < count[j]).astype(F32) * ft[rows, :].astype(F32)
        ft_f = seen
        mo[rows, :] = mo[rows, :] * ft_f
        cv[pl.ds(32 + 8 * j, 8), :] = ft_f
    sp_s[...] = jnp.zeros_like(sp_s)
    for j in range(4):
        sp_s[0:6, 8 * j : 8 * j + 8] = sp_in[:, j, :]

    pos2 = (y, x)
    at2 = (at_y, at_x)

    def chunk2(h, d, part_of):
        j = mod4(pos2[h] + d)
        return red.at[h, lax.div(j, 2), lax.rem(j, 2), pl.ds(4 * part_of, 4)]

    def msg2(h, kind, direction):
        d = 1 if direction == 0 else 3
        if kind == 0:
            src, dst = chunk2(h, 2, direction), rf2.at[h, direction]
        elif kind == 1:
            src, dst = chunk2(h, d, 1 - direction), rp2.at[h, direction]
        else:
            src, dst = chunk2(h, d, direction), rs2.at[h, direction]
        n = 6 * h + 2 * kind + direction
        return rdma(src, dst, s2.at[n], r2.at[n], at2[h](d))

    for h in range(2):
        for kind in (1, 2):
            for direction in range(2):
                msg1(h, kind, direction).wait_recv()
        mine = 4 * h + pos1[h]

        def total1(j, _, h=h, mine=mine):
            a, m = lax.div(j, 8), lax.rem(j, 8)
            red[h, 0, a, m] = part[mine, 0, a, m] + rs[h, 0, a, m] + rp[h, 1, a, m]
            red[h, 1, a, m] = part[mine, 1, a, m] + rp[h, 0, a, m] + rs[h, 1, a, m]
            return 0

        lax.fori_loop(0, 16, total1, 0)
        for direction in range(2):
            msg2(h, 0, direction).start()
        for direction in range(2):
            msg2(h, 1, direction).start()
    for h in range(2):
        for direction in range(2):
            msg2(h, 0, direction).wait_recv()
            d = 1 if direction == 0 else 3
            dst = chunk2(h, d, direction)
            for m in range(4):
                dst[m] = dst[m] + rf2[h, direction, m]
            msg2(h, 2, direction).start()

    core_to = (lax.rem(y, 2), lax.rem(x, 2))

    def msg_z(h, d):
        zt = lax.rem(z + d, 8)
        return rdma(
            zs.at[h, zt], zr.at[h, b], zsem_s.at[h], zsem_r.at[h],
            {"epoch": e, "blend": 2 * zt + core_to[h]},
        )

    for h in range(2):
        for kind in (1, 2):
            for direction in range(2):
                msg2(h, kind, direction).wait_recv()
        j = pos2[h]
        a, k = lax.div(j, 2), lax.rem(j, 2)
        for m in range(4):
            zs[h, m] = red[h, a, k, m] + rs2[h, 0, m] + rp2[h, 1, m]
            zs[h, 4 + m] = red[h, a, k, 4 + m] + rp2[h, 0, m] + rs2[h, 1, m]
        for d in (4, 3, 5, 2, 6, 1, 7):
            msg_z(h, d).start()

        @pl.when(core_to[h] == c)
        def _(h=h):
            zr[h, b] = zs[h, z]

        @pl.when(core_to[h] != c)
        def _(h=h):
            msg_z(h, 0).start()

    quantity = (lax.div(y, 2), lax.div(x, 2))
    tile = (x, 4 + y)

    def msg_x(h, d):
        et = lax.rem(e + d, 16)
        return rdma(
            zr.at[h, et], fin.at[8 * quantity[h] + tile[h]], xsem_s.at[h], xsem_r.at[h],
            {"epoch": et, "blend": b},
        )

    def wait_bytes(ref, sem):
        pltpu.make_async_copy(ref, ref, sem).wait()

    for h in range(2):

        @pl.when(core_to[h] == c)
        def _(h=h):
            wait_bytes(zr.at[h, pl.ds(0, 15)], zsem_r.at[h])
            for d in range(1, 16):
                msg_x(h, d).start()
            fin[8 * quantity[h] + tile[h]] = zr[h, e]

    for h in range(2):

        @pl.when(core_to[h] == c)
        def _(h=h):
            wait_bytes(fin.at[pl.ds(0, 7)], xsem_r.at[h])

        @pl.when(core_to[h] != c)
        def _(h=h):
            wait_bytes(fin.at[pl.ds(0, 8)], xsem_r.at[h])

    for t in range(8):
        for cpair in range(3):
            rows, lanes = slice(8 * cpair, 8 * cpair + 8), slice(128 * t, 128 * t + 128)
            wsum = fin[8 + t, cpair]
            inv = 1.0 / (1.0 + wsum)
            co[rows, lanes] = fin[t, cpair] * inv
            cv[rows, lanes] = wsum * inv
    coadd_o[...] = co[...]

    lane = lax.broadcasted_iota(jnp.int32, (8, 32), 1)
    row = lax.broadcasted_iota(jnp.int32, (8, 32), 0)
    own = (lax.div(lane, 8) == lax.rem(row, 4)).astype(F32)
    own3 = jnp.concatenate([own] * 3, axis=0)
    lane1 = lax.div(lax.broadcasted_iota(jnp.int32, (1, 32), 1), 8)
    live_row = jnp.zeros((1, 32), F32)
    for j in range(4):
        live_row = jnp.where(lane1 == j, count[j].astype(F32), live_row)
    gather = (
        lax.broadcasted_iota(jnp.int32, (8, 24), 0)
        == lax.div(lax.broadcasted_iota(jnp.int32, (8, 24), 1), 4)
    ).astype(F32)
    is_norm = row == 6
    bands = row < 6

    def dot(a, bb, ca, cb):
        return lax.dot_general(
            a, bb, (((ca,), (cb,)), ((), ())), precision=HIGHEST, preferred_element_type=F32
        )

    coadd = co[...]
    cover = cv[0:24, :]
    mask = cv[32:64, :]
    morphology = mo[...]
    spectra = sp_s[:, 0:32]
    for it in range(ITERS):
        wide = jnp.concatenate(
            [
                jnp.where(
                    row < 4,
                    jnp.broadcast_to(spectra[2 * p : 2 * p + 1], (8, 32)),
                    jnp.broadcast_to(spectra[2 * p + 1 : 2 * p + 2], (8, 32)),
                )
                for p in range(3)
            ],
            axis=0,
        ) * own3
        step = 1.0 / (1.0 + live_row * jnp.sum(spectra * spectra, axis=0, keepdims=True))
        residual = cover * (coadd - dot(wide, morphology, 1, 0))
        morphology = jnp.maximum(0.0, morphology + dot(wide * step, residual, 0, 0)) * mask
        residual = cover * (coadd - dot(wide, morphology, 1, 0))
        grad = dot(gather, dot(residual, morphology, 1, 1) * own3, 1, 0)
        norm = dot(jnp.ones((8, 1024), F32), morphology * morphology, 1, 1)
        ar[it, e] = jnp.zeros((8, LANES), F32)
        ar[it, e, :, 0:32] = jnp.where(is_norm, norm, grad)
        for d in range(1, 16):
            rdma(
                ar.at[it, e], ar.at[it, e], asem_s.at[it], asem_r.at[it],
                {"epoch": lax.rem(e + d, 16), "blend": b},
            ).start()
        if it == ITERS - 1:
            morph_o[...] = morphology
        wait_bytes(ar.at[it, pl.ds(0, 15)], asem_r.at[it])
        total = ar[it, 0, :, 0:32]
        for d in range(1, 16):
            total = total + ar[it, d, :, 0:32]
        spectra = jnp.where(
            bands,
            jnp.maximum(0.0, spectra + total / (1.0 + live_row * total[6:7])),
            0.0,
        )
    for j in range(4):
        spec_o[:, j, :] = spectra[0:6, 8 * j : 8 * j + 8]

    for h in range(2):
        for kind in range(3):
            for direction in range(2):
                msg1(h, kind, direction).wait_send()
                msg2(h, kind, direction).wait_send()

        @pl.when(core_to[h] == c)
        def _(h=h):
            wait_bytes(zs.at[h, pl.ds(0, 7)], zsem_s.at[h])
            wait_bytes(zr.at[h, pl.ds(0, 15)], xsem_s.at[h])

        @pl.when(core_to[h] != c)
        def _(h=h):
            wait_bytes(zs.at[h, pl.ds(0, 8)], zsem_s.at[h])

    for it in range(ITERS):
        wait_bytes(ar.at[it, pl.ds(0, 15)], asem_s.at[it])


def on_device(
    visit_flux, visit_precision, visit_live, footprint, source_count, spectra_init, morphology_init
):
    tile = (8, LANES)
    hbm = pl.BlockSpec(memory_space=pl.ANY)
    vmem = pl.BlockSpec(memory_space=pltpu.VMEM)
    dma = pltpu.SemaphoreType.DMA
    coadd, spectra, morphology = pl.pallas_call(
        kernel,
        name="coadd_deblend",
        out_shape=(
            jax.ShapeDtypeStruct((24, 1024), F32),
            jax.ShapeDtypeStruct((6, 4, 8), F32),
            jax.ShapeDtypeStruct((32, 1024), F32),
        ),
        in_specs=[hbm, hbm, hbm, hbm, pl.BlockSpec(memory_space=pltpu.SMEM), hbm, hbm],
        out_specs=(vmem, vmem, vmem),
        scratch_shapes=[
            pltpu.VMEM((8, 4, 6, 64, LANES), jnp.bfloat16),
            pltpu.VMEM((8, 4, 6, 64, LANES), jnp.bfloat16),
            pltpu.VMEM((4, 64), jnp.int32),
            pltpu.VMEM((4, 64, LANES), F32),
            pltpu.VMEM((32, 1024), jnp.int32),
            pltpu.VMEM((32, 1024), F32),
            pltpu.VMEM((6, 4, 8), F32),
            pltpu.VMEM(tile, F32),
            pltpu.VMEM((8, 2, 2, 8, 3, *tile), F32),
            pltpu.VMEM((2, 2, 2, 8, 3, *tile), F32),
            pltpu.VMEM((2, 2, 2, 8, 3, *tile), F32),
            pltpu.VMEM((2, 2, 2, 8, 3, *tile), F32),
            pltpu.VMEM((2, 2, 2, 8, 3, *tile), F32),
            pltpu.VMEM((2, 2, 4, 3, *tile), F32),
            pltpu.VMEM((2, 2, 4, 3, *tile), F32),
            pltpu.VMEM((2, 2, 4, 3, *tile), F32),
            pltpu.VMEM((2, 8, 3, *tile), F32),
            pltpu.VMEM((2, 16, 3, *tile), F32),
            pltpu.VMEM((16, 3, *tile), F32),
            pltpu.VMEM((24, 1024), F32),
            pltpu.VMEM((64, 1024), F32),
            pltpu.VMEM((ITERS, 16, *tile), F32),
            dma((2, 8)), dma((4,)),
            dma((12,)), dma((12,)), dma((12,)), dma((12,)),
            dma((2,)), dma((2,)), dma((2,)), dma((2,)),
            dma((ITERS,)), dma((ITERS,)),
        ],
        compiler_params=pltpu.CompilerParams(
            collective_id=0, has_side_effects=True, vmem_limit_bytes=40 * 1024 * 1024
        ),
    )(
        jnp.transpose(visit_flux, (0, 2, 1, 3)),
        jnp.transpose(visit_precision, (0, 2, 1, 3)),
        visit_live,
        footprint.reshape(32, 1024),
        source_count,
        jnp.transpose(spectra_init, (2, 0, 1)),
        morphology_init.reshape(32, 1024),
    )
    return (
        jnp.transpose(coadd.reshape(6, 4, 1024), (1, 0, 2)),
        jnp.transpose(spectra, (1, 2, 0)),
        morphology.reshape(4, 8, 1024),
    )


def solution(mesh):
    in_specs = (
        P("epoch", None, None, "blend"),
        P("epoch", None, None, "blend"),
        P("epoch", None),
        P("blend", None, "epoch"),
        P("blend"),
        P("blend", None, None),
        P("blend", None, "epoch"),
    )
    out_specs = (P("blend", None, "epoch"), P("blend", None, None), P("blend", None, "epoch"))
    return jax.shard_map(
        on_device, mesh=mesh, in_specs=in_specs, out_specs=out_specs, check_vma=False
    )
```

time: 123 us -> 67.7 us (0.55); the launches traced: 121 us -> 67.1 us
  Pallas kernels: 0 us -> 56.9 us
  blocking collectives: 55.1 us -> 0 us
  waiting for transfers between devices: 23.5 us -> 0 us
  starting transfers between devices: 17.6 us -> 0 us
  other arithmetic: 10.1 us -> 0 us
  matrix products: 2.63 us -> 0 us
  local copies, waits for them, and re-layouts: 11.3 us -> 9.54 us
    pallas_call x0 -> x1, Pallas kernels: none -> 56.9 us  [on_device(): pl.pallas_call(kernel, name='coadd_deblend', out_shape=(jax.ShapeDtypeStr...]
    all_to_all x2 -> x0, blocking collectives: 55.1 us -> none  [the longest x1 45.9 us: sent_and_summed(): lax.all_to_all(pieces, axis, split_axis=0, concat_axis=0, tiled=True)]
    all_to_all x3 -> x0, waiting for transfers between devices: 23.5 us -> none  [the longest x2 17.9 us: side_by_side_2(): lax.all_to_all(both, axis, split_axis=split_dim, concat_axis=concat_dim,...]
    all_to_all x3 -> x0, starting transfers between devices: 17.6 us -> none  [the longest x2 14.1 us: side_by_side_2(): lax.all_to_all(both, axis, split_axis=split_dim, concat_axis=concat_dim,...]
    reduce_sum x6 -> x0, other arithmetic: 5.54 us -> none  [the longest x1 5.1 us: on_device(): numerator = jnp.sum(weights * visit_flux.astype(jnp.float32), axis=0)]
    unnamed x18 -> x16, local copies, waits for them, and re-layouts: 4.22 us -> 8.87 us
    concatenate x2 -> x0, local copies, waits for them, and re-layouts: 2.88 us -> none  [the longest x1 2.37 us: side_by_side(): both = jnp.concatenate(arrays, axis=along)]
    dot_general x8 -> x0, matrix products: 2.63 us -> none  [the longest x4 1.24 us: on_device(): jnp.einsum('bkc,bkp->bcp', spectra, morphology, precision=highest)]
  transfers between devices with their start and end apart: 3 -> 0, of which waited for: 3 -> 0; matrix products, arithmetic and copies ran while one was open for 1% -> 0% of each run, Pallas kernels for 0% -> 0%
where the time goes in v1:
time: 67.7 us; the launch traced here: 67.1 us
  Pallas kernels  56.9 us (84%)
  local copies, waits for them, and re-layouts  9.54 us (14%)
    pallas_call x1, Pallas kernels, on_device(): pl.pallas_call(kernel, name='coadd_deblend', out_shape=(jax.ShapeDtypeStr...  56.9 us
    unnamed x16, local copies, waits for them, and re-layouts  8.87 us

profile of v1, /device:TPU:1, one launch (start us, length us, event | category | flops | bytes accessed | tf_op | source)
XLA Modules:
  0.0 67.1 jit_solution(2038166395517591180)
XLA Ops:
  0.6 0.0 copy-start
  0.6 1.9 %copy-done = bf16[4,64,6,1024]{3,1,2,0:T(8,128)(2,1)S(1)} copy-done((bf16[4,64,6,1024]{3,1,2,0:T(8,128)(2,1)S(1)}, bf16[4,64,6,1024]{3,1,2,0:T(8,128)(2,1)}, u32[]{:S(2)}) %copy-start) | copy-done | bytes 3145752
  2.5 0.0 copy-start.1
  2.5 1.9 %copy-done.1 = bf16[4,64,6,1024]{3,1,2,0:T(8,128)(2,1)S(1)} copy-done((bf16[4,64,6,1024]{3,1,2,0:T(8,128)(2,1)S(1)}, bf16[4,64,6,1024]{3,1,2,0:T(8,128)(2,1)}, u32[]{:S(2)}) %copy-start.1) | copy-done | bytes 3145752
  4.4 0.0 copy-start.2
  4.4 0.9 %copy-done.2 = s32[4,8,1024]{2,1,0:T(8,128)S(1)} copy-done((s32[4,8,1024]{2,1,0:T(8,128)S(1)}, s32[4,8,1024]{2,1,0:T(8,128)}, u32[]{:S(2)}) %copy-start.2) | copy-done | bytes 131096
  5.3 0.0 copy-start.3
  5.3 0.9 %copy-done.3 = f32[4,8,1024]{2,1,0:T(8,128)S(1)} copy-done((f32[4,8,1024]{2,1,0:T(8,128)S(1)}, f32[4,8,1024]{2,1,0:T(8,128)}, u32[]{:S(2)}) %copy-start.3) | copy-done | bytes 131096
  6.2 0.0 copy-start.4
  6.2 0.7 %copy-done.4 = f32[4,8,6]{1,0,2:T(4,128)S(1)} copy-done((f32[4,8,6]{1,0,2:T(4,128)S(1)}, f32[4,8,6]{1,0,2:T(4,128)}, u32[]{:S(2)}) %copy-start.4) | copy-done | bytes 792
  6.9 0.0 copy-start.5
  6.9 0.7 %copy-done.5 = s32[4,64]{1,0:T(4,128)S(1)} copy-done((s32[4,64]{1,0:T(4,128)S(1)}, s32[4,64]{1,0:T(4,128)}, u32[]{:S(2)}) %copy-start.5) | copy-done | bytes 1048
  7.6 0.0 copy-start.6
  7.6 0.7 copy-done.6
  8.3 56.9 %coadd_deblend.1 = (f32[24,1024]{1,0:T(8,128)S(1)}, f32[6,4,8]{2,1,0:T(4,128)S(1)}, f32[32,1024]{1,0:T(8,128)S(1)}) custom-call(bf16[4,6,64,1024]{3,2,1,0:T(8,128)(2,1)S(1)} %bitcast.8, bf16[4,6,64,1024]{3,2,1,0:T(8,128)(2,1)S(1)} %bitcast.9, s32[4,64]{1,0:T(4,128)S(1)} %copy-done.5, s32[32,1024]{1,0:T(8,128)S(1)} %bitcast.10, s32[4]{0:T(128)S(1)} %copy-done.6, ...), custom_call_target="tpu_custom_call" | custom-call | tf_op jit(solution)/shard_map/coadd_deblend/pallas_call | solution.py:374
  65.1 0.7 reshape.20
  65.8 0.6 copy.12
  66.4 0.7 copy.13
Async XLA Ops:
  0.6 1.9 %copy-start = (bf16[4,64,6,1024]{3,1,2,0:T(8,128)(2,1)S(1)}, bf16[4,64,6,1024]{3,1,2,0:T(8,128)(2,1)}, u32[]{:S(2)}) copy-start(bf16[4,64,6,1024]{3,1,2,0:T(8,128)(2,1)} %param.7) | copy-start | bytes 9437188
  2.5 1.9 %copy-start.1 = (bf16[4,64,6,1024]{3,1,2,0:T(8,128)(2,1)S(1)}, bf16[4,64,6,1024]{3,1,2,0:T(8,128)(2,1)}, u32[]{:S(2)}) copy-start(bf16[4,64,6,1024]{3,1,2,0:T(8,128)(2,1)} %param.8) | copy-start | bytes 9437188
  4.4 0.9 %copy-start.2 = (s32[4,8,1024]{2,1,0:T(8,128)S(1)}, s32[4,8,1024]{2,1,0:T(8,128)}, u32[]{:S(2)}) copy-start(s32[4,8,1024]{2,1,0:T(8,128)} %param.10) | copy-start | bytes 393220
  5.3 0.9 %copy-start.3 = (f32[4,8,1024]{2,1,0:T(8,128)S(1)}, f32[4,8,1024]{2,1,0:T(8,128)}, u32[]{:S(2)}) copy-start(f32[4,8,1024]{2,1,0:T(8,128)} %param.13) | copy-start | bytes 393220
  6.2 0.7 %copy-start.4 = (f32[4,8,6]{1,0,2:T(4,128)S(1)}, f32[4,8,6]{1,0,2:T(4,128)}, u32[]{:S(2)}) copy-start(f32[4,8,6]{1,0,2:T(4,128)} %param.12) | copy-start | bytes 2308
  6.9 0.7 %copy-start.5 = (s32[4,64]{1,0:T(4,128)S(1)}, s32[4,64]{1,0:T(4,128)}, u32[]{:S(2)}) copy-start(s32[4,64]{1,0:T(4,128)} %live.1) | copy-start | bytes 3076
  7.6 0.7 copy-start.6

commit v2 on v1

--- a/solution.py
+++ b/solution.py
@@ -9,14 +9,19 @@
 LANES = 128
 F32 = jnp.float32
 HIGHEST = lax.Precision.HIGHEST
+HOPS = (0, 1, 2, 1)
+FAR_FIRST = sorted(
+    [(dy, dx) for dy in range(4) for dx in range(4) if dy or dx],
+    key=lambda d: -HOPS[d[0]] - HOPS[d[1]],
+)
 
 
 def kernel(
-    flux, prec, live, foot, count, spec, morph,
+    flux, prec, live, foot, count_in, spec, morph,
     coadd_o, spec_o, morph_o,
     fx, pr, live_i, live_b, ft, mo, sp_in, sp_s,
-    part, rf, rp, rs, red, rf2, rp2, rs2, zs, zr, fin, co, cv, ar,
-    load_sem, small_sem, s1, r1, s2, r2, zsem_s, zsem_r, xsem_s, xsem_r, asem_s, asem_r,
+    part, rf, rp, rs, red, rf2, rp2, rs2, zs, fin, co, cv, ar, mout, sout,
+    count, load_sem, small_sem, ready, out_sem, s1, r1, s1s, r1s, s2, r2, zsem_s, zsem_r, asem_s, asem_r,
 ):
     e = lax.axis_index("epoch")
     b = lax.axis_index("blend")
@@ -31,12 +36,12 @@
         mod4(x + 1), mod4(x + 3), 4 + mod4(y + 1), 4 + mod4(y + 3),
         x, 4 + y,
     ]
-
     small = [
         pltpu.make_async_copy(live, live_i, small_sem.at[0]),
         pltpu.make_async_copy(spec, sp_in, small_sem.at[1]),
         pltpu.make_async_copy(foot, ft, small_sem.at[2]),
         pltpu.make_async_copy(morph, mo, small_sem.at[3]),
+        pltpu.make_async_copy(count_in, count, small_sem.at[4]),
     ]
     small[0].start()
     loads = []
@@ -46,24 +51,31 @@
             pltpu.make_async_copy(flux.at[:, :, :, lanes], fx.at[i], load_sem.at[0, i]),
             pltpu.make_async_copy(prec.at[:, :, :, lanes], pr.at[i], load_sem.at[1, i]),
         )
-        for cp in pair:
-            cp.start()
+        if i < 2:
+            for cp in pair:
+                cp.start()
         loads.append(pair)
-    for cp in small[1:]:
-        cp.start()
 
     barrier = pltpu.get_barrier_semaphore()
     for d in range(1, 16):
         pl.semaphore_signal(barrier, inc=1, device_id={"epoch": lax.rem(e + d, 16), "blend": b})
         pl.semaphore_signal(barrier, inc=1, device_id={"epoch": e, "blend": lax.rem(b + d, 16)})
-
+    for pair in loads[2:]:
+        for cp in pair:
+            cp.start()
+    for cp in small[1:]:
+        cp.start()
     small[0].wait()
     live_f = live_i[...].astype(F32)
+    pick = (
+        lax.broadcasted_iota(jnp.int32, (4, 4 * LANES), 0)
+        == lax.div(lax.broadcasted_iota(jnp.int32, (4, 4 * LANES), 1), LANES)
+    ).astype(F32)
+    spread = lax.dot_general(
+        live_f, pick, (((0,), (0,)), ((), ())), preferred_element_type=F32
+    )
     for v in range(4):
-        pick = (lax.broadcasted_iota(jnp.int32, (4, LANES), 0) == v).astype(F32)
-        live_b[v] = lax.dot_general(
-            live_f, pick, (((0,), (0,)), ((), ())), preferred_element_type=F32
-        )
+        live_b[v] = spread[:, LANES * v : LANES * v + LANES]
 
     low = lax.broadcasted_iota(jnp.int32, (8, LANES), 0) < 4
 
@@ -116,16 +128,29 @@
         d = 1 if direction == 0 else 3
         if kind == 0:
             src, dst = chunk1(h, 2, direction), rf.at[h, direction]
-        elif kind == 1:
+        else:
             src, dst = chunk1(h, d, 1 - direction), rp.at[h, direction]
-        else:
-            src, dst = chunk1(h, d, direction), rs.at[h, direction]
-        n = 6 * h + 2 * kind + direction
+        n = 4 * h + 2 * kind + direction
         return rdma(src, dst, s1.at[n], r1.at[n], at1[h](d))
 
+    pos2 = (y, x)
+    own_q = tuple(lax.div(p, 2) for p in pos2)
+    own_c = tuple(lax.rem(p, 2) for p in pos2)
+
+    def sum1(h, q, piece):
+        first = jnp.where(own_q[h] == q, 1 - own_c[h], own_c[h])
+        cc = first if piece == 0 else 1 - first
+        dev = {"epoch": jnp.where(
+            h == 0, 4 * y + mod4(x + 1 + 2 * q), 4 * mod4(y + 1 + 2 * q) + x), "blend": b}
+        return rdma(
+            part.at[4 * h + mod4(pos1[h] + 1 + 2 * q), q, cc], rs.at[h, q, cc],
+            s1s.at[h, q, piece], r1s.at[h, q, piece], dev,
+        )
     local_sums(0)
     local_sums(1)
     pl.semaphore_wait(barrier, 30)
+    for d in range(1, 16):
+        pl.semaphore_signal(ready, inc=1, device_id={"epoch": e, "blend": lax.rem(b + d, 16)})
     for h in range(2):
         for direction in range(2):
             msg1(h, 0, direction).start()
@@ -146,14 +171,13 @@
             return 0
 
         lax.fori_loop(0, 16, body, 0)
-
     for h in range(2):
         for direction in range(2):
             msg1(h, 0, direction).wait_recv()
             d = 1 if direction == 0 else 3
             add_into(chunk1(h, d, direction), rf.at[h, direction])
-            msg1(h, 2, direction).start()
-
+            for piece in range(2):
+                sum1(h, direction, piece).start()
     for cp in small[1:]:
         cp.wait()
     krow = lax.broadcasted_iota(jnp.int32, (8, 1024), 0)
@@ -167,7 +191,6 @@
     for j in range(4):
         sp_s[0:6, 8 * j : 8 * j + 8] = sp_in[:, j, :]
 
-    pos2 = (y, x)
     at2 = (at_y, at_x)
 
     def chunk2(h, d, part_of):
@@ -184,22 +207,28 @@
             src, dst = chunk2(h, d, direction), rs2.at[h, direction]
         n = 6 * h + 2 * kind + direction
         return rdma(src, dst, s2.at[n], r2.at[n], at2[h](d))
-
-    for h in range(2):
-        for kind in (1, 2):
-            for direction in range(2):
-                msg1(h, kind, direction).wait_recv()
+    def total1(h, q, cc):
         mine = 4 * h + pos1[h]
 
-        def total1(j, _, h=h, mine=mine):
-            a, m = lax.div(j, 8), lax.rem(j, 8)
-            red[h, 0, a, m] = part[mine, 0, a, m] + rs[h, 0, a, m] + rp[h, 1, a, m]
-            red[h, 1, a, m] = part[mine, 1, a, m] + rp[h, 0, a, m] + rs[h, 1, a, m]
+        def body(m, _):
+            red[h, q, cc, m] = part[mine, q, cc, m] + rs[h, q, cc, m] + rp[h, 1 - q, cc, m]
             return 0
 
-        lax.fori_loop(0, 16, total1, 0)
+        lax.fori_loop(0, 8, body, 0)
+
+    for h in range(2):
+        for direction in range(2):
+            msg1(h, 1, direction).wait_recv()
+    for h in range(2):
+        sum1(h, 1 - own_q[h], 0).wait_recv()
+        total1(h, 1 - own_q[h], own_c[h])
         for direction in range(2):
             msg2(h, 0, direction).start()
+    for h in range(2):
+        sum1(h, own_q[h], 0).wait_recv()
+        total1(h, own_q[h], 1 - own_c[h])
+        sum1(h, 1 - own_q[h], 1).wait_recv()
+        total1(h, 1 - own_q[h], 1 - own_c[h])
         for direction in range(2):
             msg2(h, 1, direction).start()
     for h in range(2):
@@ -213,17 +242,26 @@
 
     core_to = (lax.rem(y, 2), lax.rem(x, 2))
 
+    quantity = (lax.div(y, 2), lax.div(x, 2))
+    tile = (x, 4 + y)
+
+    def wait_bytes(ref, sem):
+        pltpu.make_async_copy(ref, ref, sem).wait()
+
     def msg_z(h, d):
         zt = lax.rem(z + d, 8)
         return rdma(
-            zs.at[h, zt], zr.at[h, b], zsem_s.at[h], zsem_r.at[h],
-            {"epoch": e, "blend": 2 * zt + core_to[h]},
-        )
-
+            zs.at[h, zt], fin.at[8 * quantity[h] + tile[h]], zsem_s.at[h], zsem_r.at[h],
+            {"epoch": b, "blend": 2 * zt + core_to[h]},
+        )
     for h in range(2):
         for kind in (1, 2):
             for direction in range(2):
                 msg2(h, kind, direction).wait_recv()
+        sum1(h, own_q[h], 1).wait_recv()
+        total1(h, own_q[h], own_c[h])
+        if h == 0:
+            pl.semaphore_wait(ready, 15)
         j = pos2[h]
         a, k = lax.div(j, 2), lax.rem(j, 2)
         for m in range(4):
@@ -232,46 +270,24 @@
         for d in (4, 3, 5, 2, 6, 1, 7):
             msg_z(h, d).start()
 
-        @pl.when(core_to[h] == c)
-        def _(h=h):
-            zr[h, b] = zs[h, z]
-
-        @pl.when(core_to[h] != c)
+        here = (core_to[h] == c) & (e == b)
+
+        @pl.when(here)
+        def _(h=h):
+            fin[8 * quantity[h] + tile[h]] = zs[h, z]
+
+        @pl.when(jnp.logical_not(here))
         def _(h=h):
             msg_z(h, 0).start()
-
-    quantity = (lax.div(y, 2), lax.div(x, 2))
-    tile = (x, 4 + y)
-
-    def msg_x(h, d):
-        et = lax.rem(e + d, 16)
-        return rdma(
-            zr.at[h, et], fin.at[8 * quantity[h] + tile[h]], xsem_s.at[h], xsem_r.at[h],
-            {"epoch": et, "blend": b},
-        )
-
-    def wait_bytes(ref, sem):
-        pltpu.make_async_copy(ref, ref, sem).wait()
-
-    for h in range(2):
-
-        @pl.when(core_to[h] == c)
-        def _(h=h):
-            wait_bytes(zr.at[h, pl.ds(0, 15)], zsem_r.at[h])
-            for d in range(1, 16):
-                msg_x(h, d).start()
-            fin[8 * quantity[h] + tile[h]] = zr[h, e]
-
-    for h in range(2):
-
-        @pl.when(core_to[h] == c)
-        def _(h=h):
-            wait_bytes(fin.at[pl.ds(0, 7)], xsem_r.at[h])
-
-        @pl.when(core_to[h] != c)
-        def _(h=h):
-            wait_bytes(fin.at[pl.ds(0, 8)], xsem_r.at[h])
-
+    for h in range(2):
+        here = (core_to[h] == c) & (e == b)
+        @pl.when(here)
+        def _(h=h):
+            wait_bytes(fin.at[pl.ds(0, 7)], zsem_r.at[h])
+
+        @pl.when(jnp.logical_not(here))
+        def _(h=h):
+            wait_bytes(fin.at[pl.ds(0, 8)], zsem_r.at[h])
     for t in range(8):
         for cpair in range(3):
             rows, lanes = slice(8 * cpair, 8 * cpair + 8), slice(128 * t, 128 * t + 128)
@@ -279,7 +295,8 @@
             inv = 1.0 / (1.0 + wsum)
             co[rows, lanes] = fin[t, cpair] * inv
             cv[rows, lanes] = wsum * inv
-    coadd_o[...] = co[...]
+    coadd_out = pltpu.make_async_copy(co, coadd_o, out_sem.at[0])
+    coadd_out.start()
 
     lane = lax.broadcasted_iota(jnp.int32, (8, 32), 1)
     row = lax.broadcasted_iota(jnp.int32, (8, 32), 0)
@@ -300,7 +317,6 @@
         return lax.dot_general(
             a, bb, (((ca,), (cb,)), ((), ())), precision=HIGHEST, preferred_element_type=F32
         )
-
     coadd = co[...]
     cover = cv[0:24, :]
     mask = cv[32:64, :]
@@ -326,13 +342,15 @@
         norm = dot(jnp.ones((8, 1024), F32), morphology * morphology, 1, 1)
         ar[it, e] = jnp.zeros((8, LANES), F32)
         ar[it, e, :, 0:32] = jnp.where(is_norm, norm, grad)
-        for d in range(1, 16):
+        for dy, dx in FAR_FIRST:
             rdma(
                 ar.at[it, e], ar.at[it, e], asem_s.at[it], asem_r.at[it],
-                {"epoch": lax.rem(e + d, 16), "blend": b},
+                {"epoch": 4 * mod4(y + dy) + mod4(x + dx), "blend": b},
             ).start()
         if it == ITERS - 1:
-            morph_o[...] = morphology
+            mout[...] = morphology
+            morph_out = pltpu.make_async_copy(mout, morph_o, out_sem.at[1])
+            morph_out.start()
         wait_bytes(ar.at[it, pl.ds(0, 15)], asem_r.at[it])
         total = ar[it, 0, :, 0:32]
         for d in range(1, 16):
@@ -343,25 +361,30 @@
             0.0,
         )
     for j in range(4):
-        spec_o[:, j, :] = spectra[0:6, 8 * j : 8 * j + 8]
-
-    for h in range(2):
-        for kind in range(3):
-            for direction in range(2):
+        sout[:, j, :] = spectra[0:6, 8 * j : 8 * j + 8]
+    spec_out = pltpu.make_async_copy(sout, spec_o, out_sem.at[2])
+    spec_out.start()
+    for h in range(2):
+        for direction in range(2):
+            for kind in range(2):
                 msg1(h, kind, direction).wait_send()
+                sum1(h, direction, kind).wait_send()
+            for kind in range(3):
                 msg2(h, kind, direction).wait_send()
 
-        @pl.when(core_to[h] == c)
+        here = (core_to[h] == c) & (e == b)
+        @pl.when(here)
         def _(h=h):
             wait_bytes(zs.at[h, pl.ds(0, 7)], zsem_s.at[h])
-            wait_bytes(zr.at[h, pl.ds(0, 15)], xsem_s.at[h])
-
-        @pl.when(core_to[h] != c)
+
+        @pl.when(jnp.logical_not(here))
         def _(h=h):
             wait_bytes(zs.at[h, pl.ds(0, 8)], zsem_s.at[h])
 
     for it in range(ITERS):
         wait_bytes(ar.at[it, pl.ds(0, 15)], asem_s.at[it])
+    for cp in (coadd_out, morph_out, spec_out):
+        cp.wait()
 
 
 def on_device(
@@ -369,7 +392,6 @@
 ):
     tile = (8, LANES)
     hbm = pl.BlockSpec(memory_space=pl.ANY)
-    vmem = pl.BlockSpec(memory_space=pltpu.VMEM)
     dma = pltpu.SemaphoreType.DMA
     coadd, spectra, morphology = pl.pallas_call(
         kernel,
@@ -379,8 +401,8 @@
             jax.ShapeDtypeStruct((6, 4, 8), F32),
             jax.ShapeDtypeStruct((32, 1024), F32),
         ),
-        in_specs=[hbm, hbm, hbm, hbm, pl.BlockSpec(memory_space=pltpu.SMEM), hbm, hbm],
-        out_specs=(vmem, vmem, vmem),
+        in_specs=[hbm] * 7,
+        out_specs=(hbm, hbm, hbm),
         scratch_shapes=[
             pltpu.VMEM((8, 4, 6, 64, LANES), jnp.bfloat16),
             pltpu.VMEM((8, 4, 6, 64, LANES), jnp.bfloat16),
@@ -399,18 +421,20 @@
             pltpu.VMEM((2, 2, 4, 3, *tile), F32),
             pltpu.VMEM((2, 2, 4, 3, *tile), F32),
             pltpu.VMEM((2, 8, 3, *tile), F32),
-            pltpu.VMEM((2, 16, 3, *tile), F32),
             pltpu.VMEM((16, 3, *tile), F32),
             pltpu.VMEM((24, 1024), F32),
             pltpu.VMEM((64, 1024), F32),
             pltpu.VMEM((ITERS, 16, *tile), F32),
-            dma((2, 8)), dma((4,)),
-            dma((12,)), dma((12,)), dma((12,)), dma((12,)),
-            dma((2,)), dma((2,)), dma((2,)), dma((2,)),
+            pltpu.VMEM((32, 1024), F32),
+            pltpu.VMEM((6, 4, 8), F32),
+            pltpu.SMEM((4,), jnp.int32),
+            dma((2, 8)), dma((5,)), pltpu.SemaphoreType.REGULAR, dma((3,)),
+            dma((8,)), dma((8,)), dma((2, 2, 2)), dma((2, 2, 2)), dma((12,)), dma((12,)),
+            dma((2,)), dma((2,)),
             dma((ITERS,)), dma((ITERS,)),
         ],
         compiler_params=pltpu.CompilerParams(
-            collective_id=0, has_side_effects=True, vmem_limit_bytes=40 * 1024 * 1024
+            collective_id=0, has_side_effects=True, vmem_limit_bytes=67043328
         ),
     )(
         jnp.transpose(visit_flux, (0, 2, 1, 3)),

time: 67.7 us -> 56.9 us (0.84)
  Pallas kernels: 56.9 us -> 51.7 us
  local copies, waits for them, and re-layouts: 9.54 us -> 4.44 us
    unnamed x16 -> x2, local copies, waits for them, and re-layouts: 8.87 us -> 2.87 us
    pallas_call x1, Pallas kernels: 56.9 us -> 51.7 us  [on_device(): pl.pallas_call(kernel, name='coadd_deblend', out_shape=(jax.ShapeDtypeStr...]
    reshape x1, local copies, waits for them, and re-layouts: 0.67 us -> 1.56 us  [on_device(): coadd.reshape(6, 4, 1024)]
where the time goes in v2:
time: 56.9 us; the launch traced here: 56.7 us
  Pallas kernels  51.7 us (91%)
  local copies, waits for them, and re-layouts  4.44 us (8%)
  between operations  0.64 us (1%)
    pallas_call x1, Pallas kernels, on_device(): pl.pallas_call(kernel, name='coadd_deblend', out_shape=(jax.ShapeDtypeStr...  51.7 us
    unnamed x2, local copies, waits for them, and re-layouts  2.87 us
    reshape x1, local copies, waits for them, and re-layouts, on_device(): coadd.reshape(6, 4, 1024)  1.56 us

profile of v2, /device:TPU:1, one launch (start us, length us, event | category | flops | bytes accessed | tf_op | source)
XLA Modules:
  0.0 56.7 jit_solution(9937838248527150728)
XLA Ops:
  0.6 51.7 %coadd_deblend.1 = (f32[24,1024]{1,0:T(8,128)}, f32[6,4,8]{2,1,0:T(4,128)}, f32[32,1024]{1,0:T(8,128)}) custom-call(bf16[4,6,64,1024]{3,2,1,0:T(8,128)(2,1)} %bitcast.8, bf16[4,6,64,1024]{3,2,1,0:T(8,128)(2,1)} %bitcast.9, s32[4,64]{1,0:T(4,128)} %live.1, s32[32,1024]{1,0:T(8,128)} %bitcast.10, s32[4]{0:T(128)} %count_in.1, f32[6,4,8]{2,1,0:T(4,128)} %bitcast.15, ...), custom_call_target="tpu_custom_call" | custom-call | tf_op jit(solution)/shard_map/coadd_deblend/pallas_call | solution.py:396
  52.3 1.6 %reshape.20 = f32[6,4,1024]{2,1,0:T(4,128)} reshape(f32[24,1024]{1,0:T(8,128)} %get-tuple-element.6) | data formatting | bytes 196608 | tf_op jit(solution)/shard_map/reshape | solution.py:449
  53.9 1.3 %copy.12 = f32[4,8,6]{1,0,2:T(4,128)} copy(f32[4,8,6]{1,0,2:T(4,128)} %bitcast.14) | data formatting | bytes 1536
  55.2 1.6 %copy.13 = f32[4,8,1024]{2,1,0:T(8,128)} copy(f32[4,8,1024]{2,1,0:T(8,128)} %bitcast.12) | data formatting | bytes 262144

commit v3 on v2

v3 whole, which is shorter than its diff:
```python
import jax
import jax.numpy as jnp
from jax import lax
from jax.experimental import pallas as pl
from jax.experimental.pallas import tpu as pltpu
from jax.sharding import PartitionSpec as P

ITERS = 2
LANES = 128
F32 = jnp.float32
HOPS = (0, 1, 2, 1)
FAR_FIRST = sorted(
    [(dy, dx) for dy in range(4) for dx in range(4) if dy or dx],
    key=lambda d: -HOPS[d[0]] - HOPS[d[1]],
)


def kernel(
    flux, prec, live, foot, count_in, spec, morph,
    coadd_o, spec_o, morph_o,
    fp, live_i, live_b, ft, mo, sp_in, sp_s,
    part, rf, rp, rs, red, rf2, rp2, rs2, zs, fin, co, cv, mask, mph, rsd, ar,
    count, load_sem, small_sem, waves, sent, r1, rp_sem, r1s, r2, zsem_s, zsem_r, asem_r,
):
    e = lax.axis_index("epoch")
    b = lax.axis_index("blend")
    y, x = lax.div(e, 4), lax.rem(e, 4)
    z, c = lax.div(b, 2), lax.rem(b, 2)

    def mod4(v):
        return lax.rem(v, 4)

    def wait_bytes(ref, sem):
        pltpu.make_async_copy(ref, ref, sem).wait()

    order = [
        mod4(x + 2), 4 + mod4(y + 2),
        mod4(x + 1), mod4(x + 3), 4 + mod4(y + 1), 4 + mod4(y + 3),
        x, 4 + y,
    ]
    small = [
        pltpu.make_async_copy(live, live_i, small_sem.at[0]),
        pltpu.make_async_copy(spec, sp_in, small_sem.at[1]),
        pltpu.make_async_copy(count_in, count, small_sem.at[4]),
    ]
    for t in range(8):
        lanes = pl.ds(LANES * t, LANES)
        small.append(pltpu.make_async_copy(foot.at[:, lanes], ft.at[t], small_sem.at[2]))
        small.append(pltpu.make_async_copy(morph.at[:, lanes], mo.at[t], small_sem.at[3]))
    small[0].start()
    loads = []
    for i, t in enumerate(order):
        lanes = pl.ds(pl.multiple_of(t * LANES, LANES), LANES)
        group = min(i, 2) if i < 6 else 3
        pair = (
            pltpu.make_async_copy(flux.at[:, :, :, lanes], fp.at[i, 0], load_sem.at[group]),
            pltpu.make_async_copy(prec.at[:, :, :, lanes], fp.at[i, 1], load_sem.at[group]),
        )
        if i < 2:
            for cp in pair:
                cp.start()
        loads.append(pair)

    barrier = pltpu.get_barrier_semaphore()

    def at_x(d):
        return {"epoch": 4 * y + mod4(x + d), "blend": b}

    def at_y(d):
        return {"epoch": 4 * mod4(y + d) + x, "blend": b}

    def at_z(d):
        return {"epoch": e, "blend": lax.rem(b + 2 * d, 16)}

    other_core = {"epoch": e, "blend": 2 * z + 1 - c}
    for dev in (at_x(1), at_x(3), at_y(1), at_y(3), at_z(7), other_core):
        pl.semaphore_signal(barrier, inc=1, device_id=dev)

    def wave(i):
        to = (
            (at_x(1), at_x(3)), (at_y(1), at_y(3)), (at_y(1), at_y(3)),
            (at_z(1),), (at_z(1), at_z(7)), (at_z(2), at_z(6)), (at_z(1), at_z(7)),
            (other_core,),
        )[i]
        for dev in to:
            pl.semaphore_signal(waves.at[i], inc=1, device_id=dev)
        return lambda: pl.semaphore_wait(waves.at[i], len(to))

    for pair in loads[2:]:
        for cp in pair:
            cp.start()
    for cp in small[1:]:
        cp.start()
    small[0].wait()
    live_f = live_i[...].astype(F32)
    pick = (
        lax.broadcasted_iota(jnp.int32, (4, 4 * LANES), 0)
        == lax.div(lax.broadcasted_iota(jnp.int32, (4, 4 * LANES), 1), LANES)
    ).astype(F32)
    spread = lax.dot_general(
        live_f, pick, (((0,), (0,)), ((), ())), preferred_element_type=F32
    )
    for v in range(4):
        live_b[v] = spread[:, LANES * v : LANES * v + LANES]

    low = lax.broadcasted_iota(jnp.int32, (8, LANES), 0) < 4

    def local_sums(i):
        if i in (0, 1, 2, 6):
            wait_bytes(fp.at[pl.ds(i, {2: 4, 6: 2}.get(i, 1))], load_sem.at[min(i, 3)])
        t = order[i]

        def body(g, _):
            rows = pl.ds(pl.multiple_of(g * 16, 16), 16)
            for cpair in range(3):
                sums = []
                for cc in range(2):
                    band = 2 * cpair + cc
                    num = wsum = None
                    for v in range(4):
                        w = fp[i, 1, v, band, rows, :].astype(F32) * live_b[v, rows, :]
                        n = w * fp[i, 0, v, band, rows, :].astype(F32)
                        num = n if num is None else num + n
                        wsum = w if wsum is None else wsum + w
                    sums.append((num, wsum))
                for q in range(2):
                    for zz in range(2):
                        even = sums[0][q][8 * zz : 8 * zz + 8]
                        odd = sums[1][q][8 * zz : 8 * zz + 8]
                        part[t, q, 0, 2 * g + zz, cpair] = jnp.where(low, even, pltpu.roll(odd, 4, 0))
                        part[t, q, 1, 2 * g + zz, cpair] = jnp.where(low, pltpu.roll(even, 4, 0), odd)
            return 0

        lax.fori_loop(0, 4, body, 0)

    def rdma(src, dst, ssem, rsem, dev):
        return pltpu.make_async_remote_copy(
            src, dst, ssem, rsem, device_id=dev, device_id_type=pl.DeviceIdType.MESH
        )

    pos1 = (x, y)
    at1 = (at_x, at_y)

    def chunk1(h, d, q):
        return part.at[4 * h + mod4(pos1[h] + d), q]

    def msg1(h, kind, direction):
        d = 1 if direction == 0 else 3
        if kind == 0:
            src, dst = chunk1(h, 2, direction), rf.at[h, direction]
        else:
            src, dst = chunk1(h, d, 1 - direction), rp.at[h, direction]
        arrived = rp_sem.at[0] if kind == 1 else r1.at[h, direction]
        return rdma(src, dst, sent.at[0], arrived, at1[h](d))

    pos2 = (y, x)
    own_q = tuple(lax.div(p, 2) for p in pos2)
    own_c = tuple(lax.rem(p, 2) for p in pos2)

    def sum1(h, q, piece):
        first = jnp.where(own_q[h] == q, 1 - own_c[h], own_c[h])
        cc = first if piece == 0 else 1 - first
        dev = {"epoch": jnp.where(
            h == 0, 4 * y + mod4(x + 1 + 2 * q), 4 * mod4(y + 1 + 2 * q) + x), "blend": b}
        return rdma(
            part.at[4 * h + mod4(pos1[h] + 1 + 2 * q), q, cc], rs.at[h, q, cc],
            sent.at[0], r1s.at[h, q, piece], dev,
        )
    pl.semaphore_wait(barrier, 6)
    for h in range(2):
        local_sums(h)
        for direction in range(2):
            msg1(h, 0, direction).start()
    wait_wave = wave(0)
    for i in (2, 3, 4, 5):
        local_sums(i)
        h, direction = (i - 2) // 2, (i - 2) % 2
        msg1(h, 1, direction).start()
    wait_wave()
    wait_wave = wave(1)
    local_sums(6)
    local_sums(7)
    wait_wave()
    wait_wave = wave(2)

    def add_into(dst, *srcs):
        def body(j, _):
            a, m = lax.div(j, 8), lax.rem(j, 8)
            total = dst[a, m]
            for s in srcs:
                total = total + s[a, m]
            dst[a, m] = total
            return 0

        lax.fori_loop(0, 16, body, 0)
    for h in range(2):
        for direction in range(2):
            msg1(h, 0, direction).wait_recv()
            d = 1 if direction == 0 else 3
            add_into(chunk1(h, d, direction), rf.at[h, direction])
            for piece in range(2):
                sum1(h, direction, piece).start()
    wait_wave()
    wait_wave = wave(3)
    wait_wave()
    wait_wave = wave(4)
    for cp in small[1:3]:
        cp.wait()
    wait_bytes(ft, small_sem.at[2])
    wait_bytes(mo, small_sem.at[3])
    row1 = lax.rem(lax.broadcasted_iota(jnp.int32, (8, 1), 0), 4)
    slots = jnp.zeros((8, 1), jnp.int32)
    for j in range(4):
        slots = jnp.where(row1 == j, count[j], slots)
    live_col = slots.astype(F32)

    def twice(v):
        return jnp.concatenate([v, v], axis=0)

    for k in range(8):
        rows = pl.ds(k, 4, stride=8)
        for t in range(8):
            seen = jnp.where(k < slots, twice(ft[t, rows, :].astype(F32)), 0.0)
            mask[k, t] = seen
            mph[k, t] = twice(mo[t, rows, :]) * seen
    for cpair in range(3):
        for half in range(2):
            rows_c = sp_in[2 * cpair + half]
            sp_s[4 * half : 4 * half + 4, 8 * cpair : 8 * cpair + 8] = rows_c

    at2 = (at_y, at_x)

    def msg2(h, kind, direction, piece):
        d = 1 if direction == 0 else 3
        j = mod4(pos2[h] + (2 if kind == 0 else d))
        part_of = 1 - direction if kind == 1 else direction
        dst = (rf2, rp2, rs2)[kind]
        if piece is None:
            src = red.at[h, lax.div(j, 2), lax.rem(j, 2), pl.ds(4 * part_of, 4)]
            dst, piece = dst.at[h, direction], 0
        else:
            src = red.at[h, lax.div(j, 2), lax.rem(j, 2), pl.ds(4 * part_of + 2 * piece, 2)]
            dst = dst.at[h, direction, pl.ds(2 * piece, 2)]
        arrived = rp_sem.at[1] if kind == 1 else r2.at[h, kind // 2, direction, piece]
        return rdma(src, dst, sent.at[1], arrived, at2[h](d))
    def total1(h, q, cc):
        mine = 4 * h + pos1[h]

        def body(m, _):
            red[h, q, cc, m] = part[mine, q, cc, m] + rs[h, q, cc, m] + rp[h, 1 - q, cc, m]
            return 0

        lax.fori_loop(0, 8, body, 0)

    wait_bytes(rp, rp_sem.at[0])
    wait_wave()
    wait_wave = wave(5)
    for h in range(2):
        sum1(h, 1 - own_q[h], 0).wait_recv()
        total1(h, 1 - own_q[h], own_c[h])
        for piece in range(2):
            for direction in range(2):
                msg2(h, 0, direction, piece).start()
    for h in range(2):
        sum1(h, own_q[h], 0).wait_recv()
        total1(h, own_q[h], 1 - own_c[h])
        sum1(h, 1 - own_q[h], 1).wait_recv()
        total1(h, 1 - own_q[h], 1 - own_c[h])
        for direction in range(2):
            msg2(h, 1, direction, None).start()
    wait_wave()
    wait_wave = wave(6)
    for piece in range(2):
        for h in range(2):
            for direction in range(2):
                msg2(h, 0, direction, piece).wait_recv()
                d = 1 if direction == 0 else 3
                j = mod4(pos2[h] + d)
                for m in (2 * piece, 2 * piece + 1):
                    at = (h, lax.div(j, 2), lax.rem(j, 2), 4 * direction + m)
                    red[at] = red[at] + rf2[h, direction, m]
                msg2(h, 2, direction, piece).start()
    wait_wave()
    wait_wave = wave(7)

    core_to = (lax.rem(y, 2), lax.rem(x, 2))

    quantity = (lax.div(y, 2), lax.div(x, 2))
    tile = (x, 4 + y)

    def msg_z(h, zt):
        return rdma(
            zs.at[h, zt], fin.at[8 * quantity[h] + tile[h]], zsem_s.at[h], zsem_r.at[h],
            {"epoch": b, "blend": 2 * zt + core_to[h]},
        )
    wait_bytes(rp2, rp_sem.at[1])
    here = tuple((core_to[h] == c) & (e == b) for h in range(2))
    for h in range(2):
        sum1(h, own_q[h], 1).wait_recv()
        total1(h, own_q[h], own_c[h])
    wait_wave()
    for piece in range(2):
        for h in range(2):
            for direction in range(2):
                msg2(h, 2, direction, piece).wait_recv()
                for k in (2 * piece, 2 * piece + 1):
                    m = 4 * direction + k
                    zs[h, m] = (
                        red[h, own_q[h], own_c[h], m]
                        + rs2[h, direction, k] + rp2[h, 1 - direction, k]
                    )
                    stays = here[h] & (z == m)

                    @pl.when(stays)
                    def _(h=h, m=m):
                        fin[8 * quantity[h] + tile[h]] = zs[h, m]

                    @pl.when(jnp.logical_not(stays))
                    def _(h=h, m=m):
                        msg_z(h, m).start()
    for h in range(2):

        @pl.when(here[h])
        def _(h=h):
            wait_bytes(fin.at[pl.ds(0, 7)], zsem_r.at[h])

        @pl.when(jnp.logical_not(here[h]))
        def _(h=h):
            wait_bytes(fin.at[pl.ds(0, 8)], zsem_r.at[h])
    for t in range(8):
        for cpair in range(3):
            wsum = fin[8 + t, cpair]
            inv = 1.0 / (1.0 + wsum)
            co[cpair, t] = fin[t, cpair] * inv
            cv[cpair, t] = wsum * inv
    def spread_over_pairs(v):
        return v + pltpu.roll(v, 8, 1) + pltpu.roll(v, 16, 1)

    def lanes_from(v, first):
        moved = v if first == 0 else pltpu.roll(v, 128 - first, 1)
        return jnp.where(lane128 < 8, moved, 0.0)

    lane128 = lax.broadcasted_iota(jnp.int32, (8, LANES), 1)
    spectra = jnp.where(lane128 < 24, sp_s[...], 0.0)
    for it in range(ITERS):
        power = spectra * spectra
        power = lanes_from(power, 0) + lanes_from(power, 8) + lanes_from(power, 16)
        power = power + pltpu.roll(power, 4, 0)
        step = 1.0 / (1.0 + live_col * power)
        s_of = [
            [jnp.broadcast_to(spectra[:, 8 * p + k : 8 * p + k + 1], (8, LANES)) for k in range(8)]
            for p in range(3)
        ]
        step_of = [jnp.broadcast_to(step[:, k : k + 1], (8, LANES)) for k in range(8)]

        def residual_of(planes, t):
            out = []
            for p in range(3):
                model = s_of[p][0] * planes[0]
                for k in range(1, 8):
                    model = model + s_of[p][k] * planes[k]
                out.append(cv[p, t] * (co[p, t] - model))
            return out

        for t in range(8):
            planes = [mph[k, t] for k in range(8)]
            res = residual_of(planes, t)
            for k in range(8):
                grad = s_of[0][k] * res[0] + s_of[1][k] * res[1] + s_of[2][k] * res[2]
                grad = grad + pltpu.roll(grad, 4, 0)
                planes[k] = jnp.maximum(0.0, planes[k] + grad * step_of[k]) * mask[k, t]
                mph[k, t] = planes[k]
            res = residual_of(planes, t)
            for p in range(3):
                rsd[p, t] = res[p]
        payload = jnp.zeros((8, LANES), F32)
        for k in range(8):
            sums = [None] * 4
            for t in range(8):
                plane = mph[k, t]
                terms = [plane * rsd[0, t], plane * rsd[1, t], plane * rsd[2, t], plane * plane]
                sums = [b_ if a_ is None else a_ + b_ for a_, b_ in zip(sums, terms)]
            for p in range(4):
                column = jnp.sum(sums[p], axis=1, keepdims=True)
                payload = jnp.where(lane128 == 8 * p + k, column, payload)
        ar[it, e] = payload
        for dy, dx in FAR_FIRST:
            rdma(
                ar.at[it, e], ar.at[it, e], sent.at[2], asem_r.at[it],
                {"epoch": 4 * mod4(y + dy) + mod4(x + dx), "blend": b},
            ).start()
        if it == ITERS - 1:
            for k in range(8):
                for t in range(8):
                    morph_o[t, pl.ds(k, 4, stride=8), :] = mph[k, t][0:4]
        else:
            for cpair in range(3):
                for t in range(8):
                    for half in range(2):
                        coadd_o[2 * cpair + half, :, pl.ds(LANES * t, LANES)] = co[cpair, t][
                            4 * half : 4 * half + 4
                        ]
        wait_bytes(ar.at[it, pl.ds(0, 15)], asem_r.at[it])
        total = ar[it, 0]
        for d in range(1, 16):
            total = total + ar[it, d]
        norm = spread_over_pairs(lanes_from(total, 24))
        spectra = jnp.where(
            lane128 < 24, jnp.maximum(0.0, spectra + total / (1.0 + live_col * norm)), 0.0
        )
    for cpair in range(3):
        for half in range(2):
            spec_o[2 * cpair + half] = spectra[4 * half : 4 * half + 4, 8 * cpair : 8 * cpair + 8]
    wait_bytes(part.at[pl.ds(0, 6)], sent.at[0])
    wait_bytes(part.at[pl.ds(0, 3), 0], sent.at[1])
    wait_bytes(ar.at[:, pl.ds(0, 15)], sent.at[2])
    for h in range(2):

        @pl.when(here[h])
        def _(h=h):
            wait_bytes(zs.at[h, pl.ds(0, 7)], zsem_s.at[h])

        @pl.when(jnp.logical_not(here[h]))
        def _(h=h):
            wait_bytes(zs.at[h, pl.ds(0, 8)], zsem_s.at[h])


def write_out(coadd, spectra, morphology, coadd_o, spectra_o, morphology_o, sem):
    copies = [
        pltpu.make_async_copy(
            morphology.at[t], morphology_o.at[:, pl.ds(LANES * t, LANES)], sem.at[t]
        )
        for t in range(8)
    ]
    copies.append(pltpu.make_async_copy(coadd, coadd_o, sem.at[8]))
    copies.append(pltpu.make_async_copy(spectra, spectra_o, sem.at[9]))
    for cp in copies:
        cp.start()
    for cp in copies:
        cp.wait()


def on_device(
    visit_flux, visit_precision, visit_live, footprint, source_count, spectra_init, morphology_init
):
    tile = (8, LANES)
    hbm = pl.BlockSpec(memory_space=pl.ANY)
    vmem = pl.BlockSpec(memory_space=pltpu.VMEM)
    dma = pltpu.SemaphoreType.DMA
    coadd, spectra, morphology = pl.pallas_call(
        kernel,
        name="coadd_deblend",
        out_shape=(
            jax.ShapeDtypeStruct((6, 4, 1024), F32),
            jax.ShapeDtypeStruct((6, 4, 8), F32),
            jax.ShapeDtypeStruct((8, 32, LANES), F32),
        ),
        in_specs=[hbm] * 7,
        out_specs=(vmem, vmem, vmem),
        scratch_shapes=[
            pltpu.VMEM((8, 2, 4, 6, 64, LANES), jnp.bfloat16),
            pltpu.VMEM((4, 64), jnp.int32),
            pltpu.VMEM((4, 64, LANES), F32),
            pltpu.VMEM((8, 32, LANES), jnp.int32),
            pltpu.VMEM((8, 32, LANES), F32),
            pltpu.VMEM((6, 4, 8), F32),
            pltpu.VMEM(tile, F32),
            pltpu.VMEM((8, 2, 2, 8, 3, *tile), F32),
            pltpu.VMEM((2, 2, 2, 8, 3, *tile), F32),
            pltpu.VMEM((2, 2, 2, 8, 3, *tile), F32),
            pltpu.VMEM((2, 2, 2, 8, 3, *tile), F32),
            pltpu.VMEM((2, 2, 2, 8, 3, *tile), F32),
            pltpu.VMEM((2, 2, 4, 3, *tile), F32),
            pltpu.VMEM((2, 2, 4, 3, *tile), F32),
            pltpu.VMEM((2, 2, 4, 3, *tile), F32),
            pltpu.VMEM((2, 8, 3, *tile), F32),
            pltpu.VMEM((16, 3, *tile), F32),
            pltpu.VMEM((3, 8, *tile), F32),
            pltpu.VMEM((3, 8, *tile), F32),
            pltpu.VMEM((8, 8, *tile), F32),
            pltpu.VMEM((8, 8, *tile), F32),
            pltpu.VMEM((3, 8, *tile), F32),
            pltpu.VMEM((ITERS, 16, *tile), F32),
            pltpu.SMEM((4,), jnp.int32),
            dma((4,)), dma((5,)), pltpu.SemaphoreType.REGULAR((8,)),
            dma((3,)), dma((2, 2)), dma((2,)), dma((2, 2, 2)), dma((2, 2, 2, 2)),
            dma((2,)), dma((2,)), dma((ITERS,)),
        ],
        compiler_params=pltpu.CompilerParams(
            collective_id=0, has_side_effects=True, vmem_limit_bytes=48 * 1024 * 1024
        ),
    )(
        *[
            pltpu.with_memory_space_constraint(a, pltpu.HBM)
            for a in (
                jnp.transpose(visit_flux, (0, 2, 1, 3)),
                jnp.transpose(visit_precision, (0, 2, 1, 3)),
                visit_live,
                footprint.reshape(32, 1024),
                source_count,
                jnp.transpose(spectra_init, (2, 0, 1)),
                morphology_init.reshape(32, 1024),
            )
        ]
    )
    coadd, spectra, morphology = pl.pallas_call(
        write_out,
        name="write_out",
        out_shape=(
            jax.ShapeDtypeStruct((6, 4, 1024), F32),
            jax.ShapeDtypeStruct((6, 4, 8), F32),
            jax.ShapeDtypeStruct((32, 1024), F32),
        ),
        in_specs=[vmem, vmem, vmem],
        out_specs=(hbm, hbm, hbm),
        scratch_shapes=[dma((10,))],
        compiler_params=pltpu.CompilerParams(vmem_limit_bytes=1024 * 1024),
    )(coadd, spectra, morphology)
    return (
        jnp.transpose(coadd, (1, 0, 2)),
        jnp.transpose(spectra, (1, 2, 0)),
        morphology.reshape(4, 8, 1024),
    )


def solution(mesh):
    in_specs = (
        P("epoch", None, None, "blend"),
        P("epoch", None, None, "blend"),
        P("epoch", None),
        P("blend", None, "epoch"),
        P("blend"),
        P("blend", None, None),
        P("blend", None, "epoch"),
    )
    out_specs = (P("blend", None, "epoch"), P("blend", None, None), P("blend", None, "epoch"))
    return jax.shard_map(
        on_device, mesh=mesh, in_specs=in_specs, out_specs=out_specs, check_vma=False
    )
```

time: 56.9 us -> 48.4 us (0.85)
  the two profiles are of different devices: /device:TPU:1 before, /device:TPU:64 now
where the time goes in v3:
time: 48.4 us; the launch traced here: 48.3 us
  Pallas kernels  47.7 us (99%)
  between operations  0.64 us (1%)
    pallas_call x1, Pallas kernels, on_device(): pl.pallas_call(kernel, name='coadd_deblend', out_shape=(jax.ShapeDtypeStr...  46.9 us

profile of v3, /device:TPU:64, one launch (start us, length us, event | category | flops | bytes accessed | tf_op | source)
XLA Modules:
  0.0 48.3 jit_solution(14078661209966619429)
XLA Ops:
  0.6 46.9 %coadd_deblend.1 = (f32[6,4,1024]{2,1,0:T(4,128)S(1)}, f32[6,4,8]{2,1,0:T(4,128)S(1)}, f32[8,32,128]{2,1,0:T(8,128)S(1)}) custom-call(bf16[4,6,64,1024]{3,2,1,0:T(8,128)(2,1)} %bitcast.8, bf16[4,6,64,1024]{3,2,1,0:T(8,128)(2,1)} %bitcast.9, s32[4,64]{1,0:T(4,128)} %live.1, s32[32,1024]{1,0:T(8,128)} %bitcast.10, s32[4]{0:T(128)} %count_in.1, ...), custom_call_target="tpu_custom_call" | custom-call | tf_op jit(solution)/shard_map/coadd_deblend/pallas_call | solution.py:450
  47.6 0.8 %write_out.1 = (f32[6,4,1024]{2,1,0:T(4,128)}, f32[6,4,8]{2,1,0:T(4,128)}, f32[32,1024]{1,0:T(8,128)}) custom-call(f32[6,4,1024]{2,1,0:T(4,128)S(1)} %get-tuple-element.9.coadd, f32[6,4,8]{2,1,0:T(4,128)S(1)} %get-tuple-element.10.spectra, f32[8,32,128]{2,1,0:T(8,128)S(1)} %get-tuple-element.11.morphology), custom_call_target="tpu_custom_call" | custom-call | tf_op jit(solution)/shard_map/write_out/pallas_call | solution.py:506

commit v4 on v3

--- a/solution.py
+++ b/solution.py
@@ -8,6 +8,7 @@
 ITERS = 2
 LANES = 128
 F32 = jnp.float32
+AWAY = ((4, 2, 6, 0), (3, 5, 1, 7))
 HOPS = (0, 1, 2, 1)
 FAR_FIRST = sorted(
     [(dy, dx) for dy in range(4) for dx in range(4) if dy or dx],
@@ -20,7 +21,7 @@
     coadd_o, spec_o, morph_o,
     fp, live_i, live_b, ft, mo, sp_in, sp_s,
     part, rf, rp, rs, red, rf2, rp2, rs2, zs, fin, co, cv, mask, mph, rsd, ar,
-    count, load_sem, small_sem, waves, sent, r1, rp_sem, r1s, r2, zsem_s, zsem_r, asem_r,
+    count, load_sem, small_sem, waves, sent, r1, rp_sem, r1s, r2, zsem_r, asem_r,
 ):
     e = lax.axis_index("epoch")
     b = lax.axis_index("blend")
@@ -105,6 +106,21 @@
 
     low = lax.broadcasted_iota(jnp.int32, (8, LANES), 0) < 4
 
+    pos2 = (y, x)
+    goal2 = (lax.div(z, 2), 2 * lax.rem(z, 2) + c)
+
+    def look_up(values, i):
+        out = values[0]
+        for k in range(1, len(values)):
+            out = jnp.where(i == k, values[k], out)
+        return out
+
+    def slot_of(h, q, d):
+        chunk = 2 * q + lax.rem(goal2[h] + 1 + d, 2)
+        return look_up((3, 1, 0, 2), mod4(chunk - pos2[h] + 4))
+
+    halves = (0, 1, 0, 0, 1, 1, 0, 1)
+
     def local_sums(i):
         if i in (0, 1, 2, 6):
             wait_bytes(fp.at[pl.ds(i, {2: 4, 6: 2}.get(i, 1))], load_sem.at[min(i, 3)])
@@ -112,6 +128,9 @@
 
         def body(g, _):
             rows = pl.ds(pl.multiple_of(g * 16, 16), 16)
+            steps = [lax.rem(2 * g + zz - z + 8, 8) for zz in range(2)]
+            slots = [[slot_of(halves[i], q, d) for d in steps] for q in range(2)]
+            nths = [look_up([AWAY[k % 2].index(k) for k in range(8)], d) for d in steps]
             for cpair in range(3):
                 sums = []
                 for cc in range(2):
@@ -127,8 +146,9 @@
                     for zz in range(2):
                         even = sums[0][q][8 * zz : 8 * zz + 8]
                         odd = sums[1][q][8 * zz : 8 * zz + 8]
-                        part[t, q, 0, 2 * g + zz, cpair] = jnp.where(low, even, pltpu.roll(odd, 4, 0))
-                        part[t, q, 1, 2 * g + zz, cpair] = jnp.where(low, pltpu.roll(even, 4, 0), odd)
+                        s, n, w = slots[q][zz], lax.rem(nths[zz], 2), lax.div(nths[zz], 2)
+                        part[t, 0, s, n, w, cpair] = jnp.where(low, even, pltpu.roll(odd, 4, 0))
+                        part[t, 1, s, n, w, cpair] = jnp.where(low, pltpu.roll(even, 4, 0), odd)
             return 0
 
         lax.fori_loop(0, 4, body, 0)
@@ -153,18 +173,13 @@
         arrived = rp_sem.at[0] if kind == 1 else r1.at[h, direction]
         return rdma(src, dst, sent.at[0], arrived, at1[h](d))
 
-    pos2 = (y, x)
-    own_q = tuple(lax.div(p, 2) for p in pos2)
-    own_c = tuple(lax.rem(p, 2) for p in pos2)
+    PIECES = ((0, 1), (1, 2), (3, 1))
 
     def sum1(h, q, piece):
-        first = jnp.where(own_q[h] == q, 1 - own_c[h], own_c[h])
-        cc = first if piece == 0 else 1 - first
-        dev = {"epoch": jnp.where(
-            h == 0, 4 * y + mod4(x + 1 + 2 * q), 4 * mod4(y + 1 + 2 * q) + x), "blend": b}
+        slots = pl.ds(*PIECES[piece])
         return rdma(
-            part.at[4 * h + mod4(pos1[h] + 1 + 2 * q), q, cc], rs.at[h, q, cc],
-            sent.at[0], r1s.at[h, q, piece], dev,
+            part.at[4 * h + mod4(pos1[h] + 1 + 2 * q), q, slots], rs.at[h, q, slots],
+            sent.at[0], r1s.at[h, q, piece], at1[h](1 + 2 * q),
         )
     pl.semaphore_wait(barrier, 6)
     for h in range(2):
@@ -183,16 +198,13 @@
     wait_wave()
     wait_wave = wave(2)
 
-    def add_into(dst, *srcs):
+    def add_into(dst, src):
         def body(j, _):
-            a, m = lax.div(j, 8), lax.rem(j, 8)
-            total = dst[a, m]
-            for s in srcs:
-                total = total + s[a, m]
-            dst[a, m] = total
+            a, n = lax.div(j, 2), lax.rem(j, 2)
+            dst[a, n] = dst[a, n] + src[a, n]
             return 0
 
-        lax.fori_loop(0, 16, body, 0)
+        lax.fori_loop(0, 8, body, 0)
     for h in range(2):
         for direction in range(2):
             msg1(h, 0, direction).wait_recv()
@@ -232,106 +244,91 @@
 
     def msg2(h, kind, direction, piece):
         d = 1 if direction == 0 else 3
-        j = mod4(pos2[h] + (2 if kind == 0 else d))
-        part_of = 1 - direction if kind == 1 else direction
-        dst = (rf2, rp2, rs2)[kind]
-        if piece is None:
-            src = red.at[h, lax.div(j, 2), lax.rem(j, 2), pl.ds(4 * part_of, 4)]
-            dst, piece = dst.at[h, direction], 0
+        slot = 0 if kind == 0 else 1 + direction
+        if kind == 1:
+            src, dst = red.at[h, slot, 1 - direction], rp2.at[h, direction]
+            arrived = rp_sem.at[1]
         else:
-            src = red.at[h, lax.div(j, 2), lax.rem(j, 2), pl.ds(4 * part_of + 2 * piece, 2)]
-            dst = dst.at[h, direction, pl.ds(2 * piece, 2)]
-        arrived = rp_sem.at[1] if kind == 1 else r2.at[h, kind // 2, direction, piece]
+            src = red.at[h, slot, direction, piece]
+            dst = (rf2, None, rs2)[kind].at[h, direction, piece]
+            arrived = r2.at[h, kind // 2, direction, piece]
         return rdma(src, dst, sent.at[1], arrived, at2[h](d))
-    def total1(h, q, cc):
+    def total1(h, slot):
         mine = 4 * h + pos1[h]
 
-        def body(m, _):
-            red[h, q, cc, m] = part[mine, q, cc, m] + rs[h, q, cc, m] + rp[h, 1 - q, cc, m]
+        def body(j, _):
+            n, w = lax.div(j, 2), lax.rem(j, 2)
+            for q in range(2):
+                red[h, slot, n, w, q] = (
+                    part[mine, q, slot, n, w] + rs[h, q, slot, n, w] + rp[h, 1 - q, slot, n, w]
+                )
             return 0
 
-        lax.fori_loop(0, 8, body, 0)
+        lax.fori_loop(0, 4, body, 0)
 
     wait_bytes(rp, rp_sem.at[0])
     wait_wave()
     wait_wave = wave(5)
     for h in range(2):
-        sum1(h, 1 - own_q[h], 0).wait_recv()
-        total1(h, 1 - own_q[h], own_c[h])
+        for q in range(2):
+            sum1(h, q, 0).wait_recv()
+        total1(h, 0)
         for piece in range(2):
             for direction in range(2):
                 msg2(h, 0, direction, piece).start()
     for h in range(2):
-        sum1(h, own_q[h], 0).wait_recv()
-        total1(h, own_q[h], 1 - own_c[h])
-        sum1(h, 1 - own_q[h], 1).wait_recv()
-        total1(h, 1 - own_q[h], 1 - own_c[h])
+        for q in range(2):
+            sum1(h, q, 2).start()
+    wait_wave()
+    wait_wave = wave(6)
+    for h in range(2):
+        for q in range(2):
+            sum1(h, q, 1).wait_recv()
+        for slot in (1, 2):
+            total1(h, slot)
         for direction in range(2):
             msg2(h, 1, direction, None).start()
-    wait_wave()
-    wait_wave = wave(6)
     for piece in range(2):
         for h in range(2):
             for direction in range(2):
                 msg2(h, 0, direction, piece).wait_recv()
-                d = 1 if direction == 0 else 3
-                j = mod4(pos2[h] + d)
-                for m in (2 * piece, 2 * piece + 1):
-                    at = (h, lax.div(j, 2), lax.rem(j, 2), 4 * direction + m)
-                    red[at] = red[at] + rf2[h, direction, m]
+                at = (h, 1 + direction, direction, piece)
+                red[at] = red[at] + rf2[h, direction, piece]
                 msg2(h, 2, direction, piece).start()
     wait_wave()
     wait_wave = wave(7)
 
-    core_to = (lax.rem(y, 2), lax.rem(x, 2))
-
-    quantity = (lax.div(y, 2), lax.div(x, 2))
-    tile = (x, 4 + y)
-
-    def msg_z(h, zt):
+    place = (2 * x + lax.div(y, 2), 2 * (4 + y) + lax.div(x, 2))
+    odd = [lax.rem(pos2[h] + goal2[h] + 1, 2) for h in range(2)]
+
+    def msg_z(h, n, w, core):
+        d = look_up((AWAY[0][2 * w + n], AWAY[1][2 * w + n]), odd[h])
         return rdma(
-            zs.at[h, zt], fin.at[8 * quantity[h] + tile[h]], zsem_s.at[h], zsem_r.at[h],
-            {"epoch": b, "blend": 2 * zt + core_to[h]},
+            zs.at[h, n, w, core], fin.at[place[h]], sent.at[3], zsem_r.at[0],
+            {"epoch": b, "blend": 2 * lax.rem(z + d, 8) + core},
         )
+    for h in range(2):
+        for q in range(2):
+            sum1(h, q, 2).wait_recv()
+        total1(h, 3)
+    wait_wave()
     wait_bytes(rp2, rp_sem.at[1])
-    here = tuple((core_to[h] == c) & (e == b) for h in range(2))
-    for h in range(2):
-        sum1(h, own_q[h], 1).wait_recv()
-        total1(h, own_q[h], own_c[h])
-    wait_wave()
     for piece in range(2):
         for h in range(2):
-            for direction in range(2):
-                msg2(h, 2, direction, piece).wait_recv()
-                for k in (2 * piece, 2 * piece + 1):
-                    m = 4 * direction + k
-                    zs[h, m] = (
-                        red[h, own_q[h], own_c[h], m]
-                        + rs2[h, direction, k] + rp2[h, 1 - direction, k]
+            for n in range(2):
+                msg2(h, 2, n, piece).wait_recv()
+                for core in range(2):
+                    zs[h, n, piece, core] = (
+                        red[h, 3, n, piece, core]
+                        + rs2[h, n, piece, core] + rp2[h, 1 - n, piece, core]
                     )
-                    stays = here[h] & (z == m)
-
-                    @pl.when(stays)
-                    def _(h=h, m=m):
-                        fin[8 * quantity[h] + tile[h]] = zs[h, m]
-
-                    @pl.when(jnp.logical_not(stays))
-                    def _(h=h, m=m):
-                        msg_z(h, m).start()
-    for h in range(2):
-
-        @pl.when(here[h])
-        def _(h=h):
-            wait_bytes(fin.at[pl.ds(0, 7)], zsem_r.at[h])
-
-        @pl.when(jnp.logical_not(here[h]))
-        def _(h=h):
-            wait_bytes(fin.at[pl.ds(0, 8)], zsem_r.at[h])
+                    msg_z(h, n, piece, core).start()
+    wait_bytes(fin, zsem_r.at[0])
     for t in range(8):
         for cpair in range(3):
-            wsum = fin[8 + t, cpair]
+            wsum = fin[2 * t + 1, cpair]
             inv = 1.0 / (1.0 + wsum)
-            co[cpair, t] = fin[t, cpair] * inv
+            co[cpair, t] = fin[2 * t, cpair] * inv
             cv[cpair, t] = wsum * inv
     def spread_over_pairs(v):
         return v + pltpu.roll(v, 8, 1) + pltpu.roll(v, 16, 1)
@@ -414,15 +411,7 @@
     wait_bytes(part.at[pl.ds(0, 6)], sent.at[0])
     wait_bytes(part.at[pl.ds(0, 3), 0], sent.at[1])
     wait_bytes(ar.at[:, pl.ds(0, 15)], sent.at[2])
-    for h in range(2):
-
-        @pl.when(here[h])
-        def _(h=h):
-            wait_bytes(zs.at[h, pl.ds(0, 7)], zsem_s.at[h])
-
-        @pl.when(jnp.logical_not(here[h]))
-        def _(h=h):
-            wait_bytes(zs.at[h, pl.ds(0, 8)], zsem_s.at[h])
+    wait_bytes(zs, sent.at[3])
 
 
 def write_out(coadd, spectra, morphology, coadd_o, spectra_o, morphology_o, sem):
@@ -465,15 +454,15 @@
             pltpu.VMEM((8, 32, LANES), F32),
             pltpu.VMEM((6, 4, 8), F32),
             pltpu.VMEM(tile, F32),
-            pltpu.VMEM((8, 2, 2, 8, 3, *tile), F32),
-            pltpu.VMEM((2, 2, 2, 8, 3, *tile), F32),
-            pltpu.VMEM((2, 2, 2, 8, 3, *tile), F32),
-            pltpu.VMEM((2, 2, 2, 8, 3, *tile), F32),
-            pltpu.VMEM((2, 2, 2, 8, 3, *tile), F32),
-            pltpu.VMEM((2, 2, 4, 3, *tile), F32),
-            pltpu.VMEM((2, 2, 4, 3, *tile), F32),
-            pltpu.VMEM((2, 2, 4, 3, *tile), F32),
-            pltpu.VMEM((2, 8, 3, *tile), F32),
+            pltpu.VMEM((8, 2, 4, 2, 2, 3, *tile), F32),
+            pltpu.VMEM((2, 2, 4, 2, 2, 3, *tile), F32),
+            pltpu.VMEM((2, 2, 4, 2, 2, 3, *tile), F32),
+            pltpu.VMEM((2, 2, 4, 2, 2, 3, *tile), F32),
+            pltpu.VMEM((2, 4, 2, 2, 2, 3, *tile), F32),
+            pltpu.VMEM((2, 2, 2, 2, 3, *tile), F32),
+            pltpu.VMEM((2, 2, 2, 2, 3, *tile), F32),
+            pltpu.VMEM((2, 2, 2, 2, 3, *tile), F32),
+            pltpu.VMEM((2, 2, 2, 2, 3, *tile), F32),
             pltpu.VMEM((16, 3, *tile), F32),
             pltpu.VMEM((3, 8, *tile), F32),
             pltpu.VMEM((3, 8, *tile), F32),
@@ -483,8 +472,8 @@
             pltpu.VMEM((ITERS, 16, *tile), F32),
             pltpu.SMEM((4,), jnp.int32),
             dma((4,)), dma((5,)), pltpu.SemaphoreType.REGULAR((8,)),
-            dma((3,)), dma((2, 2)), dma((2,)), dma((2, 2, 2)), dma((2, 2, 2, 2)),
-            dma((2,)), dma((2,)), dma((ITERS,)),
+            dma((4,)), dma((2, 2)), dma((2,)), dma((2, 2, 3)), dma((2, 2, 2, 2)),
+            dma((1,)), dma((ITERS,)),
         ],
         compiler_params=pltpu.CompilerParams(
             collective_id=0, has_side_effects=True, vmem_limit_bytes=48 * 1024 * 1024

time: 48.4 us -> 46.6 us (0.963)
  the two profiles are of different devices: /device:TPU:64 before, /device:TPU:1 now
where the time goes in v4:
time: 46.6 us; the launch traced here: 46.5 us
  Pallas kernels  45.9 us (98%)
  between operations  0.64 us (1%)
    pallas_call x1, Pallas kernels, on_device(): pl.pallas_call(kernel, name='coadd_deblend', out_shape=(jax.ShapeDtypeStr...  45.1 us

profile of v4, /device:TPU:1, one launch (start us, length us, event | category | flops | bytes accessed | tf_op | source)
XLA Modules:
  0.0 46.5 jit_solution(10193483091252466607)
XLA Ops:
  0.6 45.1 %coadd_deblend.1 = (f32[6,4,1024]{2,1,0:T(4,128)S(1)}, f32[6,4,8]{2,1,0:T(4,128)S(1)}, f32[8,32,128]{2,1,0:T(8,128)S(1)}) custom-call(bf16[4,6,64,1024]{3,2,1,0:T(8,128)(2,1)} %bitcast.8, bf16[4,6,64,1024]{3,2,1,0:T(8,128)(2,1)} %bitcast.9, s32[4,64]{1,0:T(4,128)} %live.1, s32[32,1024]{1,0:T(8,128)} %bitcast.10, s32[4]{0:T(128)} %count_in.1, ...), custom_call_target="tpu_custom_call" | custom-call | tf_op jit(solution)/shard_map/coadd_deblend/pallas_call | solution.py:439
  45.7 0.8 %write_out.1 = (f32[6,4,1024]{2,1,0:T(4,128)}, f32[6,4,8]{2,1,0:T(4,128)}, f32[32,1024]{1,0:T(8,128)}) custom-call(f32[6,4,1024]{2,1,0:T(4,128)S(1)} %get-tuple-element.9.coadd, f32[6,4,8]{2,1,0:T(4,128)S(1)} %get-tuple-element.10.spectra, f32[8,32,128]{2,1,0:T(8,128)S(1)} %get-tuple-element.11.morphology), custom_call_target="tpu_custom_call" | custom-call | tf_op jit(solution)/shard_map/write_out/pallas_call | solution.py:495

commit v5 on v4

--- a/solution.py
+++ b/solution.py
@@ -298,13 +298,14 @@
     wait_wave()
     wait_wave = wave(7)
 
+    tile = (x, 4 + y)
     place = (2 * x + lax.div(y, 2), 2 * (4 + y) + lax.div(x, 2))
     odd = [lax.rem(pos2[h] + goal2[h] + 1, 2) for h in range(2)]
 
     def msg_z(h, n, w, core):
         d = look_up((AWAY[0][2 * w + n], AWAY[1][2 * w + n]), odd[h])
         return rdma(
-            zs.at[h, n, w, core], fin.at[place[h]], sent.at[3], zsem_r.at[0],
+            zs.at[h, n, w, core], fin.at[place[h]], sent.at[3], zsem_r.at[tile[h]],
             {"epoch": b, "blend": 2 * lax.rem(z + d, 8) + core},
         )
     for h in range(2):
@@ -323,13 +324,16 @@
                         + rs2[h, n, piece, core] + rp2[h, 1 - n, piece, core]
                     )
                     msg_z(h, n, piece, core).start()
-    wait_bytes(fin, zsem_r.at[0])
-    for t in range(8):
+    arrivals = [first + mod4(at + d) for d in (0, 1, 3, 2) for first, at in ((0, x), (4, y))]
+
+    def take(t):
+        wait_bytes(fin.at[pl.ds(2 * t, 2)], zsem_r.at[t])
         for cpair in range(3):
             wsum = fin[2 * t + 1, cpair]
             inv = 1.0 / (1.0 + wsum)
             co[cpair, t] = fin[2 * t, cpair] * inv
             cv[cpair, t] = wsum * inv
+
     def spread_over_pairs(v):
         return v + pltpu.roll(v, 8, 1) + pltpu.roll(v, 16, 1)
 
@@ -338,6 +342,8 @@
         return jnp.where(lane128 < 8, moved, 0.0)
 
     lane128 = lax.broadcasted_iota(jnp.int32, (8, LANES), 1)
+    row128 = lax.broadcasted_iota(jnp.int32, (8, LANES), 0)
+    offset = lane128 - 32 * lax.rem(row128, 4)
     spectra = jnp.where(lane128 < 24, sp_s[...], 0.0)
     for it in range(ITERS):
         power = spectra * spectra
@@ -359,7 +365,9 @@
                 out.append(cv[p, t] * (co[p, t] - model))
             return out
 
-        for t in range(8):
+        for t in arrivals if it == 0 else range(8):
+            if it == 0:
+                take(t)
             planes = [mph[k, t] for k in range(8)]
             res = residual_of(planes, t)
             for k in range(8):
@@ -379,8 +387,11 @@
                 sums = [b_ if a_ is None else a_ + b_ for a_, b_ in zip(sums, terms)]
             for p in range(4):
                 column = jnp.sum(sums[p], axis=1, keepdims=True)
-                payload = jnp.where(lane128 == 8 * p + k, column, payload)
-        ar[it, e] = payload
+                payload = jnp.where(offset == 8 * p + k, column, payload)
+        payload = payload + pltpu.roll(payload, 1, 0)
+        payload = payload + pltpu.roll(payload, 2, 0)
+        ar[it, e, 0:1] = payload[3:4]
+        ar[it, e, 1:2] = payload[7:8]
         for dy, dx in FAR_FIRST:
             rdma(
                 ar.at[it, e], ar.at[it, e], sent.at[2], asem_r.at[it],
@@ -398,9 +409,17 @@
                             4 * half : 4 * half + 4
                         ]
         wait_bytes(ar.at[it, pl.ds(0, 15)], asem_r.at[it])
-        total = ar[it, 0]
+        packed = ar[it, 0]
         for d in range(1, 16):
-            total = total + ar[it, d]
+            packed = packed + ar[it, d]
+        both = jnp.where(
+            row128 < 4,
+            jnp.broadcast_to(packed[0:1], (8, LANES)),
+            jnp.broadcast_to(packed[1:2], (8, LANES)),
+        )
+        total = both
+        for r in range(1, 4):
+            total = jnp.where(lax.rem(row128, 4) == r, pltpu.roll(both, LANES - 32 * r, 1), total)
         norm = spread_over_pairs(lanes_from(total, 24))
         spectra = jnp.where(
             lane128 < 24, jnp.maximum(0.0, spectra + total / (1.0 + live_col * norm)), 0.0
@@ -469,11 +488,11 @@
             pltpu.VMEM((8, 8, *tile), F32),
             pltpu.VMEM((8, 8, *tile), F32),
             pltpu.VMEM((3, 8, *tile), F32),
-            pltpu.VMEM((ITERS, 16, *tile), F32),
+            pltpu.VMEM((ITERS, 16, 2, LANES), F32),
             pltpu.SMEM((4,), jnp.int32),
             dma((4,)), dma((5,)), pltpu.SemaphoreType.REGULAR((8,)),
             dma((4,)), dma((2, 2)), dma((2,)), dma((2, 2, 3)), dma((2, 2, 2, 2)),
-            dma((1,)), dma((ITERS,)),
+            dma((8,)), dma((ITERS,)),
         ],
         compiler_params=pltpu.CompilerParams(
             collective_id=0, has_side_effects=True, vmem_limit_bytes=48 * 1024 * 1024

time: 46.6 us -> 46.6 us (level)
  no operation moved by 1% of the time
where the time goes in v5:
time: 46.6 us; the launch traced here: 46.5 us
  Pallas kernels  45.8 us (98%)
  between operations  0.64 us (1%)
    pallas_call x1, Pallas kernels, on_device(): pl.pallas_call(kernel, name='coadd_deblend', out_shape=(jax.ShapeDtypeStr...  45.1 us

profile of v5, /device:TPU:1, one launch (start us, length us, event | category | flops | bytes accessed | tf_op | source)
XLA Modules:
  0.0 46.5 jit_solution(6004290005541857485)
XLA Ops:
  0.6 45.1 %coadd_deblend.1 = (f32[6,4,1024]{2,1,0:T(4,128)S(1)}, f32[6,4,8]{2,1,0:T(4,128)S(1)}, f32[8,32,128]{2,1,0:T(8,128)S(1)}) custom-call(bf16[4,6,64,1024]{3,2,1,0:T(8,128)(2,1)} %bitcast.8, bf16[4,6,64,1024]{3,2,1,0:T(8,128)(2,1)} %bitcast.9, s32[4,64]{1,0:T(4,128)} %live.1, s32[32,1024]{1,0:T(8,128)} %bitcast.10, s32[4]{0:T(128)} %count_in.1, ...), custom_call_target="tpu_custom_call" | custom-call | tf_op jit(solution)/shard_map/coadd_deblend/pallas_call | solution.py:458
  45.7 0.8 %write_out.1 = (f32[6,4,1024]{2,1,0:T(4,128)}, f32[6,4,8]{2,1,0:T(4,128)}, f32[32,1024]{1,0:T(8,128)}) custom-call(f32[6,4,1024]{2,1,0:T(4,128)S(1)} %get-tuple-element.9.coadd, f32[6,4,8]{2,1,0:T(4,128)S(1)} %get-tuple-element.10.spectra, f32[8,32,128]{2,1,0:T(8,128)S(1)} %get-tuple-element.11.morphology), custom_call_target="tpu_custom_call" | custom-call | tf_op jit(solution)/shard_map/write_out/pallas_call | solution.py:514
